TPU v7x, 128 devices: a whole 4x4x4 slice. The times are simulated.
128 devices in a mesh: seq: 64 (over z_hi, x, y, core), head: 2 (over z_lo).
Axes of the slice: x: 4, y: 4, z: 4 (z_hi: 2, z_lo: 2; z = z_hi * 2 + z_lo), core: 2. Of those that a mesh axis runs over, the one named last changes fastest.
Arguments:
- tokens: bfloat16 [32768, 3584], P('seq', 'head'), may hold values from -6 to 6
- pre_gain: float32 [3584], replicated, may hold values from 0.5 to 1.5
- query_weight: bfloat16 [3584, 2048], P(None, 'head'), may hold values from -0.375 to 0.375
- key_weight: bfloat16 [3584, 1024], P(None, 'head'), may hold values from -0.375 to 0.375
- value_weight: bfloat16 [3584, 1024], P(None, 'head'), may hold values from -0.09375 to 0.09375
- out_weight: bfloat16 [2048, 3584], P('head'), may hold values from -0.5 to 0.5
- post_gain: float32 [3584], P('head'), may hold values from 0.5 to 1.5
Outputs:
- layer_out: bfloat16 [32768, 3584], P('seq', 'head')
All inputs are finite; a program needn't handle non-finite values.
Results may differ from a plain program's by a relative error of at most 0.013.
The roundings to bfloat16 on the way count: a program that leaves them out, or rounds other values in their place, can miss the bound.
Values may be sent and summed in bfloat16 or wider, within the bound.
A program may use at most 192 MiB of HBM per device.

v0:
```python
import functools
import math

import jax
import jax.numpy as jnp
from jax import lax
from jax.experimental import pallas as pl
from jax.experimental.pallas import tpu as pltpu
from jax.sharding import PartitionSpec as P

D = 3584
HALF = 1792
HD = 256
ROWS = 512
CHUNKS = 4
PART = ROWS // CHUNKS
SLOTS = 9
MESH = pl.DeviceIdType.MESH
F32 = jnp.float32
BF16 = jnp.bfloat16
softcap_limit = 50.0
rope_base = 10000.0
norm_epsilon = 1e-06


def place():
    s = lax.axis_index("seq")
    head = lax.axis_index("head")
    core = lax.rem(s, 2)
    chip = lax.div(s, 2)
    y = lax.rem(chip, 4)
    return s, head, core, chip, y


def rope_tables(row_count):
    positions = lax.axis_index("seq") * row_count + jnp.arange(row_count, dtype=jnp.int32)
    frequency = jnp.exp(-jnp.log(rope_base) * (2.0 * jnp.arange(HD // 2, dtype=F32) / HD))
    angles = positions.astype(F32)[:, None] * frequency[None, :]
    return jnp.cos(angles), jnp.sin(angles)


def slot_rows(slot, chunk):
    return pl.ds(pl.multiple_of((SLOTS - 1 - slot) * ROWS + chunk * PART, PART), PART)


def qkv_kernel(
    tok, gain, wq, wk, wv, cosine, sine, q_out, kv,
    xbuf, xn, wqb, wkb, wvb, load_sem, z_send, z_recv, send, recv, pair_send, pair_recv,
):
    s, head, core, chip, y = place()
    seq_up = s + jnp.where(y < 3, 2, -6)
    seq_down = s + jnp.where(y > 0, -2, 6)
    sibling = s + 1 - 2 * core
    has_next = chip < 28
    has_prev = chip >= 4

    def at_seq(target):
        return (target, head)

    loads = [
        pltpu.make_async_copy(tok, xbuf.at[head], load_sem.at[0]),
        pltpu.make_async_copy(wk, wkb, load_sem.at[1]),
        pltpu.make_async_copy(wv, wvb, load_sem.at[2]),
        pltpu.make_async_copy(wq, wqb, load_sem.at[3]),
    ]
    for load in loads:
        load.start()

    barrier = pltpu.get_barrier_semaphore()
    for target in (at_seq(sibling), (s, 1 - head), at_seq(seq_up), at_seq(seq_down)):
        pl.semaphore_signal(barrier, inc=1, device_id=target, device_id_type=MESH)

    @pl.when(has_next)
    def _():
        pl.semaphore_signal(barrier, inc=1, device_id=at_seq(s + 8), device_id_type=MESH)

    @pl.when(has_prev)
    def _():
        pl.semaphore_signal(barrier, inc=1, device_id=at_seq(s - 8), device_id_type=MESH)

    pl.semaphore_wait(barrier, 4 + has_next.astype(jnp.int32) + has_prev.astype(jnp.int32))

    def token_copy(i):
        rows = pl.ds(pl.multiple_of(i * PART, PART), PART)
        return pltpu.make_async_remote_copy(
            src_ref=tok.at[rows],
            dst_ref=xbuf.at[head, rows],
            send_sem=z_send.at[i],
            recv_sem=z_recv.at[i],
            device_id=(s, 1 - head),
            device_id_type=MESH,
        )

    def token_arrival(i):
        rows = pl.ds(pl.multiple_of(i * PART, PART), PART)
        return pltpu.make_async_remote_copy(
            src_ref=tok.at[rows],
            dst_ref=xbuf.at[1 - head, rows],
            send_sem=z_send.at[i],
            recv_sem=z_recv.at[i],
            device_id=(s, 1 - head),
            device_id_type=MESH,
        )

    def flow(index, i, source, slot, target):
        return pltpu.make_async_remote_copy(
            src_ref=kv.at[slot_rows(source, i)],
            dst_ref=kv.at[slot_rows(slot, i)],
            send_sem=send.at[index, i],
            recv_sem=recv.at[index, i],
            device_id=at_seq(target),
            device_id_type=MESH,
        )

    def far(i):
        return flow(0, i, 0, 8, s + 8)

    def up(i):
        return flow(1, i, jnp.where(y < 3, 0, 8), 2, seq_up)

    def down(i):
        return flow(2, i, jnp.where(y == 0, 0, 8), 6, seq_down)

    def second_up(i):
        return flow(3, i, 2, 4, seq_up)

    def second_down(i):
        return pltpu.make_async_remote_copy(
            src_ref=kv.at[slot_rows(6, i)],
            dst_ref=kv.at[slot_rows(4, i)],
            send_sem=send.at[4, i],
            recv_sem=recv.at[3, i],
            device_id=at_seq(seq_down),
            device_id_type=MESH,
        )

    def to_sibling(i, slot):
        target = slot + 1 - 2 * core
        lane = lax.div(target - 1, 2)
        return pltpu.make_async_remote_copy(
            src_ref=kv.at[slot_rows(slot, i)],
            dst_ref=kv.at[slot_rows(target, i)],
            send_sem=pair_send.at[lane, i],
            recv_sem=pair_recv.at[lane, i],
            device_id=at_seq(sibling),
            device_id_type=MESH,
        )

    def when(condition, action):
        pl.when(condition)(action)

    up_own = y < 3
    up_relay = (y == 3) & has_prev
    down_own = y == 0
    down_relay = (y > 0) & has_prev
    second_up_valid = (y < 3) & (chip >= 1)
    second_down_valid = (y == 1) & has_prev

    for i in range(CHUNKS):
        token_copy(i).start()
    for load in loads:
        load.wait()

    def roped(values, rows):
        cos = cosine[rows]
        sin = sine[rows]
        leading = values[:, : HD // 2]
        trailing = values[:, HD // 2 :]
        return jnp.concatenate([leading * cos - trailing * sin, trailing * cos + leading * sin], axis=1).astype(BF16)

    def own(i):
        token_arrival(i).wait_recv()
        rows = pl.ds(pl.multiple_of(i * PART, PART), PART)
        first = xbuf[0, rows].astype(F32)
        second = xbuf[1, rows].astype(F32)
        squares = jnp.sum(first * first, axis=-1, keepdims=True) + jnp.sum(second * second, axis=-1, keepdims=True)
        scale = lax.rsqrt(squares / D + norm_epsilon)
        xn[:, :HALF] = (first * scale * gain[:, :HALF]).astype(BF16)
        xn[:, HALF:] = (second * scale * gain[:, HALF:]).astype(BF16)

        def key(j, carry):
            columns = pl.ds(pl.multiple_of(j * HD, HD), HD)
            out = jnp.dot(xn[...], wkb[:, columns], preferred_element_type=F32)
            kv[slot_rows(0, i), columns] = roped(out, rows)
            return carry

        def value(j, carry):
            columns = pl.ds(pl.multiple_of(j * HD, HD), HD)
            out = jnp.dot(xn[...], wvb[:, columns], preferred_element_type=F32)
            kv[slot_rows(0, i), pl.ds(pl.multiple_of(2 * HD + j * HD, HD), HD)] = out.astype(BF16)
            return carry

        def query(j, carry):
            columns = pl.ds(pl.multiple_of(j * HD, HD), HD)
            out = jnp.dot(xn[...], wqb[:, columns], preferred_element_type=F32)
            q_out[j, rows] = roped(out, rows)
            return carry

        lax.fori_loop(0, 2, value, 0)
        lax.fori_loop(0, 2, key, 0)
        when(has_next, lambda: far(i).start())
        when(up_own, lambda: up(i).start())
        when(down_own, lambda: down(i).start())
        when(core == 0, lambda: to_sibling(i, 0).start())
        lax.fori_loop(0, 4, query, 0)

    def relay_far(i):
        @pl.when(has_prev)
        def _():
            far(i).wait_recv()
            when(up_relay, lambda: up(i).start())
            when(down_relay, lambda: down(i).start())
            when(core == 1, lambda: to_sibling(i, 8).start())

    def relay_near(i):
        @pl.when(chip >= 1)
        def _():
            up(i).wait_recv()
            when(second_up_valid, lambda: second_up(i).start())
            to_sibling(i, 2).start()

        @pl.when(chip >= 3)
        def _():
            down(i).wait_recv()
            when(second_down_valid, lambda: second_down(i).start())
            to_sibling(i, 6).start()

    def relay_second(i):
        @pl.when(chip >= 2)
        def _():
            second_up(i).wait_recv()
            to_sibling(i, 4).start()

    def step(i, carry):
        @pl.when(i < CHUNKS)
        def _():
            own(i)

        @pl.when((i >= 1) & (i < CHUNKS + 1))
        def _():
            relay_far(i - 1)

        @pl.when((i >= 2) & (i < CHUNKS + 2))
        def _():
            relay_near(i - 2)

        @pl.when(i >= 3)
        def _():
            relay_second(i - 3)

        return carry

    lax.fori_loop(0, CHUNKS + 3, step, 0)

    def drain(i, carry):
        token_copy(i).wait_send()
        when(has_next, lambda: far(i).wait_send())
        when(up_own | up_relay, lambda: up(i).wait_send())
        when(down_own | down_relay, lambda: down(i).wait_send())
        when(second_up_valid, lambda: second_up(i).wait_send())
        when(second_down_valid, lambda: second_down(i).wait_send())
        for slot in (0, 2, 4, 6, 8):
            sends = (slot <= s) & ((core == 0) if slot == 0 else (core == 1) if slot == 8 else (core >= 0))
            when(sends, lambda: to_sibling(i, slot).wait_send())
        for lane in range(4):
            @pl.when(s >= 2 * lane + 1)
            def _():
                pltpu.make_async_remote_copy(
                    src_ref=kv.at[slot_rows(0, i)],
                    dst_ref=kv.at[slot_rows(2 * lane + 1, i)],
                    send_sem=pair_send.at[lane, i],
                    recv_sem=pair_recv.at[lane, i],
                    device_id=at_seq(sibling),
                    device_id_type=MESH,
                ).wait_recv()
        return carry

    lax.fori_loop(0, CHUNKS, drain, 0)


EXP_SCALE = softcap_limit * math.log2(math.e)
SCORE_SCALE = HD ** (-0.5) / softcap_limit
TILE = 256


def attention_kernel(q, kv, out, acc, den):
    s = lax.axis_index("seq")

    def unit(u, carry):
        group = lax.div(u, 2)
        tile = lax.rem(u, 2)
        key_columns = pl.ds(pl.multiple_of(group * HD, HD), HD)
        value_columns = pl.ds(pl.multiple_of(2 * HD + group * HD, HD), HD)
        query = q[pl.ds(2 * group, 2), pl.ds(pl.multiple_of(tile * TILE, TILE), TILE)].reshape(2 * TILE, HD)

        def block(index, count, mask):
            rows = pl.ds(pl.multiple_of(index * TILE, TILE), count * TILE)
            scores = lax.dot_general(
                query, kv[rows, key_columns], (((1,), (1,)), ((), ())), preferred_element_type=F32
            )
            weights = jnp.exp2(EXP_SCALE * jnp.tanh(scores * SCORE_SCALE))
            if mask is not None:
                weights = jnp.where(mask, weights, 0.0)
            partial = weights[:, :128]
            for part in range(1, count * 2):
                partial = partial + weights[:, part * 128 : (part + 1) * 128]
            product = jnp.dot(weights.astype(BF16), kv[rows, value_columns], preferred_element_type=F32)
            return partial, product

        query_row = lax.rem(lax.broadcasted_iota(jnp.int32, (2 * TILE, TILE), 0), TILE)
        key_row = lax.broadcasted_iota(jnp.int32, (2 * TILE, TILE), 1)
        partial, product = block(16 + tile, 1, key_row <= query_row)
        den[...] = partial
        acc[...] = product

        @pl.when(s >= 8)
        def _():
            partial, product = block(tile, 1, key_row > query_row)
            den[...] += partial
            acc[...] += product

        total = jnp.minimum(15, 2 * s + tile)
        groups = lax.div(total, 3)

        def triple(j, carry):
            partial, product = block(13 + tile - 3 * j, 3, None)
            den[...] += partial
            acc[...] += product
            return carry

        def single(j, carry):
            partial, product = block(15 + tile - 3 * groups - j, 1, None)
            den[...] += partial
            acc[...] += product
            return carry

        lax.fori_loop(0, groups, triple, 0)
        lax.fori_loop(0, total - 3 * groups, single, 0)
        denominator = jnp.sum(den[...], axis=-1, keepdims=True)
        attended = (acc[...] / denominator).astype(BF16)
        rows = pl.ds(pl.multiple_of(tile * TILE, TILE), TILE)
        for member in range(2):
            columns = pl.ds(pl.multiple_of((2 * group + member) * HD, HD), HD)
            out[rows, columns] = attended[member * TILE : (member + 1) * TILE]
        return carry

    lax.fori_loop(0, 4, unit, 0)


def in_blocks(shard, dim, length):
    before, after = (shard.shape[:dim], shard.shape[dim + 1 :])
    return jnp.moveaxis(shard.reshape(*before, length, -1, *after), dim, 0)


def local(tokens, pre_gain, query_weight, key_weight, value_weight, out_weight, post_gain):
    cosine, sine = rope_tables(ROWS)
    vmem = pl.BlockSpec(memory_space=pltpu.VMEM)
    hbm = pl.BlockSpec(memory_space=pl.ANY)
    dma = pltpu.SemaphoreType.DMA
    queries, keys_values = pl.pallas_call(
        qkv_kernel,
        out_shape=(
            jax.ShapeDtypeStruct((4, ROWS, HD), BF16),
            jax.ShapeDtypeStruct((SLOTS * ROWS, 4 * HD), BF16),
        ),
        in_specs=[hbm, vmem, hbm, hbm, hbm, vmem, vmem],
        out_specs=(vmem, vmem),
        scratch_shapes=[
            pltpu.VMEM((2, ROWS, HALF), BF16),
            pltpu.VMEM((PART, D), BF16),
            pltpu.VMEM((D, 4 * HD), BF16),
            pltpu.VMEM((D, 2 * HD), BF16),
            pltpu.VMEM((D, 2 * HD), BF16),
            dma((4,)),
            dma((CHUNKS,)),
            dma((CHUNKS,)),
            dma((5, CHUNKS)),
            dma((4, CHUNKS)),
            dma((4, CHUNKS)),
            dma((4, CHUNKS)),
        ],
        compiler_params=pltpu.CompilerParams(
            collective_id=0, has_side_effects=True, vmem_limit_bytes=60 * 1024 * 1024
        ),
        name="qkv",
    )(tokens, pre_gain[None, :], query_weight, key_weight, value_weight, cosine, sine)
    attended = pl.pallas_call(
        attention_kernel,
        out_shape=jax.ShapeDtypeStruct((ROWS, 4 * HD), BF16),
        in_specs=[vmem, vmem],
        out_specs=vmem,
        scratch_shapes=[pltpu.VMEM((2 * TILE, HD), F32), pltpu.VMEM((2 * TILE, 128), F32)],
        compiler_params=pltpu.CompilerParams(vmem_limit_bytes=60 * 1024 * 1024),
        name="attention",
    )(queries, keys_values)
    partial_branch = jnp.dot(attended, out_weight, preferred_element_type=F32)
    blocks = in_blocks(partial_branch.astype(BF16), 1, 2)
    arrived = lax.all_to_all(blocks, "head", split_axis=0, concat_axis=0, tiled=True)
    share = arrived.astype(F32).sum(axis=0)
    squares = lax.all_gather(jnp.sum(share * share, axis=1, keepdims=True), "head").sum(0)
    inverse_rms = lax.rsqrt(squares / D + norm_epsilon)
    return (tokens.astype(F32) + post_gain * share * inverse_rms).astype(BF16)


def solution(mesh):
    placed = (
        P("seq", "head"),
        P(),
        P(None, "head"),
        P(None, "head"),
        P(None, "head"),
        P("head", None),
        P("head"),
    )
    return jax.shard_map(
        local, mesh=mesh, in_specs=placed, out_specs=P("seq", "head"), check_vma=False
    )
```

profile of v0, /device:TPU:2, one launch (start us, length us, event | category | flops | bytes accessed | tf_op | source)
XLA Modules:
  0.0 189.5 jit_solution(7769775001057349941)
XLA Ops:
  0.0 1.3 broadcast_in_dim.2.gain
  1.4 1.8 multiply_sine_fusion
  3.1 98.5 %qkv.1 = (bf16[4,512,256]{2,1,0:T(8,128)(2,1)}, bf16[4608,1024]{1,0:T(8,128)(2,1)}) custom-call(bf16[512,1792]{1,0:T(8,128)(2,1)} %tok.1, f32[1,3584]{1,0:T(1,128)} %broadcast_in_dim.2.gain, bf16[3584,1024]{1,0:T(8,128)(2,1)} %wq.1, bf16[3584,512]{1,0:T(8,128)(2,1)} %wk.1, bf16[3584,512]{1,0:T(8,128)(2,1)} %wv.1, f32[512,128]{1,0:T(8,128)} %get-tuple-element.10.cosine, ...), custom_call_target="tpu_custom_call" | custom-call | tf_op jit(solution)/shard_map/qkv/pallas_call | solution.py:360
  101.6 23.9 %attention.1 = bf16[512,1024]{1,0:T(8,128)(2,1)} custom-call(bf16[4,512,256]{2,1,0:T(8,128)(2,1)} %get-tuple-element.7.q, bf16[4608,1024]{1,0:T(8,128)(2,1)} %get-tuple-element.8.kv), custom_call_target="tpu_custom_call" | custom-call | tf_op jit(solution)/shard_map/attention/pallas_call | solution.py:387
  125.6 7.4 %convolution_convert_fusion = bf16[512,3584]{1,0:T(8,128)(2,1)S(1)} fusion(bf16[512,1024]{1,0:T(8,128)(2,1)} %attention.1, bf16[1024,3584]{1,0:T(8,128)(2,1)} %param.12), kind=kOutput, calls=%fused_computation.1 | convolution fusion | flops 3759931392 | bytes 12058624 | tf_op jit(solution)/shard_map/dot_general | solution.py:396
  132.9 0.2 copy.11
  133.2 45.2 %all_to_all.5 = bf16[2,512,1792]{2,1,0:T(8,128)(2,1)S(1)} all-to-all(bf16[2,512,1792]{2,1,0:T(8,128)(2,1)S(1)} %bitcast.10), channel_id=1, replica_groups=mesh['seq'=64,'head'=2] {'head'}, dimensions={0} | all-to-all | bytes 7340032 | tf_op jit(solution)/shard_map/all_to_all | solution.py:398
  178.4 0.6 convert_reduce_fusion
  179.0 0.0 copy-start
  179.0 1.8 copy-done
  180.8 0.0 copy-start.1
  180.8 0.0 copy-start.2
  180.8 0.3 multiply_reduce_fusion
  181.1 4.5 %all-gather.1 = f32[2,1,512]{2,1,0:T(1,128)S(1)} all-gather(f32[1,1,512]{2,1,0:T(1,128)S(1)} %bitcast.12), channel_id=2, replica_groups=mesh['seq'=64,'head'=2] {'head'}, dimensions={0}, use_global_device_ids=true | all-gather | bytes 6144 | tf_op jit(solution)/shard_map/all_gather | solution.py:400
  185.7 0.0 copy-done.1
  185.7 0.0 copy-done.2
  185.7 3.9 %add_convert_fusion = bf16[512,1792]{1,0:T(8,128)(2,1)} fusion(f32[512,1792]{1,0:T(8,128)} %copy-done, bf16[512,1792]{1,0:T(8,128)(2,1)S(1)} %copy-done.1, f32[512]{0:T(512)S(1)} %add_rsqrt_fusion, f32[1792]{0:T(1024)S(1)} %copy-done.2), kind=kLoop, calls=%fused_computation.3 | loop fusion | flops 4587520 | bytes 7349248 | tf_op jit(solution)/shard_map/convert_element_type | solution.py:402
  (4 shorter events, 0.0 us)
Async XLA Ops:
  179.0 1.8 copy-start
  180.8 4.8 %copy-start.1 = (bf16[512,1792]{1,0:T(8,128)(2,1)S(1)}, bf16[512,1792]{1,0:T(8,128)(2,1)}, u32[]{:S(2)}) copy-start(bf16[512,1792]{1,0:T(8,128)(2,1)} %tok.1) | copy-start | bytes 5505028
  180.8 4.9 %copy-start.2 = (f32[1792]{0:T(1024)S(1)}, f32[1792]{0:T(1024)}, u32[]{:S(2)}) copy-start(f32[1792]{0:T(1024)} %param.13) | copy-start | bytes 21508
where the time goes:
time: 190 us
  Pallas kernels  122 us (64%)
  blocking collectives  49.7 us (26%)
  matrix products  7.38 us (4%)
  other arithmetic  6.62 us (3%)
  local copies, waits for them, and re-layouts  3.36 us (2%)
    pallas_call x1, Pallas kernels, local(): pl.pallas_call(qkv_kernel, out_shape=(jax.ShapeDtypeStruct((4, ROWS, HD),...  98.5 us
    all_to_all x1, blocking collectives, local(): lax.all_to_all(blocks, 'head', split_axis=0, concat_axis=0, tiled=True)  45.2 us
    pallas_call x1, Pallas kernels, local(): pl.pallas_call(attention_kernel, out_shape=jax.ShapeDtypeStruct((ROWS, 4...  23.9 us
    dot_general x1, matrix products, local(): partial_branch = jnp.dot(attended, out_weight, preferred_element_type=F32)  7.38 us
    all_gather x1, blocking collectives, local(): lax.all_gather(jnp.sum(share * share, axis=1, keepdims=True), 'head').sum(0)  4.5 us
    convert_element_type x1, other arithmetic, local(): return (tokens.astype(F32) + post_gain * share * inverse_rms).astype(BF16)  3.85 us

commit v1 on v0

v1 whole, which is shorter than its diff:
```python
import math

import jax
import jax.numpy as jnp
from jax import lax
from jax.experimental import pallas as pl
from jax.experimental.pallas import tpu as pltpu
from jax.sharding import PartitionSpec as P

D = 3584
HALF = 1792
HD = 256
ROWS = 512
CHUNKS = 8
PART = ROWS // CHUNKS
SLOTS = 9
TILE = 256
UNITS = 4
MESH = pl.DeviceIdType.MESH
F32 = jnp.float32
BF16 = jnp.bfloat16
softcap_limit = 50.0
rope_base = 10000.0
norm_epsilon = 1e-06
EXP_SCALE = softcap_limit * math.log2(math.e)
SCORE_SCALE = HD ** (-0.5) / softcap_limit


def rope_tables(row_count):
    positions = lax.axis_index("seq") * row_count + jnp.arange(row_count, dtype=jnp.int32)
    frequency = jnp.exp(-jnp.log(rope_base) * (2.0 * jnp.arange(HD // 2, dtype=F32) / HD))
    angles = positions.astype(F32)[:, None] * frequency[None, :]
    return jnp.cos(angles), jnp.sin(angles)


def aligned(start, size, step=None):
    return pl.ds(pl.multiple_of(start, step or size), size)


def slot_rows(slot, chunk):
    return aligned((SLOTS - 1 - slot) * ROWS + chunk * PART, PART)


def when(condition, action):
    pl.when(condition)(action)


def layer_kernel(
    tok, gain, wq, wk, wv, wo, post, cosine, sine, out,
    xbuf, xn, wqb, wkb, wvb, wob, q, kv, acc, den, att, branch, transit, sums, obuf,
    load_sem, z_send, z_recv, send, recv, pair_send, pair_recv,
    transit_send, transit_recv, onward_send, w_send, w_recv, att_send, att_recv, sum_send, sum_recv, out_sem,
):
    s = lax.axis_index("seq")
    head = lax.axis_index("head")
    core = lax.rem(s, 2)
    chip = lax.div(s, 2)
    y = lax.rem(chip, 4)
    x = lax.rem(lax.div(chip, 4), 4)
    z = lax.div(chip, 16)
    other = 1 - head
    seq_up = s + jnp.where(y < 3, 2, -6)
    seq_down = s + jnp.where(y > 0, -2, 6)
    sibling = s + 1 - 2 * core
    has_next = chip < 28
    has_prev = chip >= 4
    crosses = (z == 0) & (x == 3)
    ring_y = [s + 2 * (lax.rem(y + k, 4) - y) for k in (1, 2, 3)]
    ring_x = [s + 8 * (lax.rem(x + k, 4) - x) for k in (1, 2, 3)]

    def at_seq(target):
        return (target, head)

    partner = (s, other)

    def remote(source, target, send_sem, recv_sem, device):
        return pltpu.make_async_remote_copy(
            src_ref=source, dst_ref=target, send_sem=send_sem, recv_sem=recv_sem,
            device_id=device, device_id_type=MESH,
        )

    own_columns = aligned(head * HALF, HALF, 128)
    other_columns = aligned(other * HALF, HALF, 128)
    loads = [
        pltpu.make_async_copy(tok, xbuf.at[head], load_sem.at[0]),
        pltpu.make_async_copy(wv, wvb, load_sem.at[1]),
        pltpu.make_async_copy(wk, wkb, load_sem.at[2]),
        pltpu.make_async_copy(wq, wqb, load_sem.at[3]),
        pltpu.make_async_copy(wo.at[:, own_columns], wob.at[aligned(head * 1024, 1024)], load_sem.at[4]),
    ]
    for load in loads:
        load.start()

    barrier = pltpu.get_barrier_semaphore()

    def greet(device):
        pl.semaphore_signal(barrier, inc=1, device_id=device, device_id_type=MESH)

    greet(partner)
    greet(at_seq(sibling))
    for target in ring_y + ring_x:
        greet(at_seq(target))

    @pl.when(z == 1)
    def _():
        greet(at_seq((12 + y) * 2 + core))

    @pl.when(crosses)
    def _():
        for column in range(4):
            greet(at_seq((16 + 4 * column + y) * 2 + core))

    pl.semaphore_wait(barrier, 8 + z + 4 * crosses.astype(jnp.int32))

    slice_index = (core * 4 + x) * 4 + y
    mine = head * 1024
    theirs = other * 1024

    def weight_slice():
        return remote(
            wo.at[aligned(slice_index * 32, 32), other_columns], wob.at[aligned(mine + slice_index * 32, 32)],
            w_send.at[0], w_recv.at[0], partner,
        )

    def weight_along_y(k):
        rows = aligned(theirs + slice_index * 32, 32)
        return remote(wob.at[rows], wob.at[rows], w_send.at[1 + k], w_recv.at[1 + k], at_seq(ring_y[k]))

    def weight_along_x(k):
        rows = aligned(theirs + (core * 4 + x) * 128, 128)
        return remote(wob.at[rows], wob.at[rows], w_send.at[4 + k], w_recv.at[4 + k], at_seq(ring_x[k]))

    def weight_sibling():
        rows = aligned(theirs + core * 512, 512)
        return remote(wob.at[rows], wob.at[rows], w_send.at[7], w_recv.at[7], at_seq(sibling))

    def token_copy(i):
        rows = aligned(i * PART, PART)
        return remote(tok.at[rows], xbuf.at[head, rows], z_send.at[i], z_recv.at[i], partner)

    def token_arrival(i):
        rows = aligned(i * PART, PART)
        return remote(tok.at[rows], xbuf.at[other, rows], z_send.at[i], z_recv.at[i], partner)

    def flow(index, i, source, slot, target):
        return remote(
            kv.at[slot_rows(source, i)], kv.at[slot_rows(slot, i)], send.at[index, i], recv.at[index, i], at_seq(target)
        )

    def far(i):
        return flow(0, i, 0, 8, s + 8)

    def far_transit(i):
        column = lax.rem(i, 4)
        return remote(
            kv.at[slot_rows(0, i)], transit.at[lax.div(i, 4)], transit_send.at[i], transit_recv.at[lax.div(i, 4)],
            at_seq((16 + 4 * column + y) * 2 + core),
        )

    def onward(i):
        return remote(
            transit.at[lax.div(i, 4)], kv.at[slot_rows(8, i)], onward_send.at[lax.div(i, 4)], recv.at[0, i], at_seq(s - 8 * x)
        )

    def far_direct(i):
        return has_next & ((z == 1) | (x < 3) | (lax.rem(i, 4) == 0))

    def far_by_transit(i):
        return crosses & (lax.rem(i, 4) > 0)

    def onward_here(i):
        return (z == 1) & (x > 0) & (lax.rem(i, 4) == x)

    def up(i):
        return flow(1, i, jnp.where(y < 3, 0, 8), 2, seq_up)

    def down(i):
        return flow(2, i, jnp.where(y == 0, 0, 8), 6, seq_down)

    def second_up(i):
        return flow(3, i, 2, 4, seq_up)

    def second_down(i):
        return remote(
            kv.at[slot_rows(6, i)], kv.at[slot_rows(4, i)], send.at[4, i], recv.at[3, i], at_seq(seq_down)
        )

    def to_sibling(i, slot):
        target = slot + 1 - 2 * core
        lane = lax.div(target - 1, 2)
        return remote(
            kv.at[slot_rows(slot, i)], kv.at[slot_rows(target, i)], pair_send.at[lane, i], pair_recv.at[lane, i],
            at_seq(sibling),
        )

    up_own = y < 3
    up_relay = (y == 3) & has_prev
    down_own = y == 0
    down_relay = (y > 0) & has_prev
    second_up_valid = (y < 3) & (chip >= 1)
    second_down_valid = (y == 1) & has_prev

    weight_slice().start()
    for i in range(CHUNKS):
        token_copy(i).start()
    for load in loads[:4]:
        load.wait()
    weight_slice().wait_recv()
    for k in range(3):
        weight_along_y(k).start()

    def roped(values, rows):
        cos = cosine[rows]
        sin = sine[rows]
        leading = values[:, : HD // 2]
        trailing = values[:, HD // 2 :]
        return jnp.concatenate([leading * cos - trailing * sin, trailing * cos + leading * sin], axis=1).astype(BF16)

    def own(i):
        token_arrival(i).wait_recv()
        rows = aligned(i * PART, PART)
        first = xbuf[0, rows].astype(F32)
        second = xbuf[1, rows].astype(F32)
        squares = jnp.sum(first * first, axis=-1, keepdims=True) + jnp.sum(second * second, axis=-1, keepdims=True)
        scale = lax.rsqrt(squares / D + norm_epsilon)
        xn[:, :HALF] = (first * scale * gain[:, :HALF]).astype(BF16)
        xn[:, HALF:] = (second * scale * gain[:, HALF:]).astype(BF16)

        def key(j, carry):
            columns = aligned(j * HD, HD)
            product = jnp.dot(xn[...], wkb[:, columns], preferred_element_type=F32)
            kv[slot_rows(0, i), columns] = roped(product, rows)
            return carry

        def value(j, carry):
            product = jnp.dot(xn[...], wvb[:, aligned(j * HD, HD)], preferred_element_type=F32)
            kv[slot_rows(0, i), aligned(2 * HD + j * HD, HD)] = product.astype(BF16)
            return carry

        def query(j, carry):
            product = jnp.dot(xn[...], wqb[:, aligned(j * HD, HD)], preferred_element_type=F32)
            q[j, rows] = roped(product, rows)
            return carry

        lax.fori_loop(0, 2, value, 0)
        lax.fori_loop(0, 2, key, 0)
        when(far_direct(i), lambda: far(i).start())
        when(far_by_transit(i), lambda: far_transit(i).start())
        when(up_own, lambda: up(i).start())
        when(down_own, lambda: down(i).start())
        when(core == 0, lambda: to_sibling(i, 0).start())
        lax.fori_loop(0, 4, query, 0)

    def relay_onward(i):
        @pl.when(onward_here(i))
        def _():
            far_transit(i).wait_recv()
            onward(i).start()

    def relay_far(i):
        @pl.when(has_prev)
        def _():
            far(i).wait_recv()
            when(up_relay, lambda: up(i).start())
            when(down_relay, lambda: down(i).start())
            when(core == 1, lambda: to_sibling(i, 8).start())

    def relay_near(i):
        @pl.when(chip >= 1)
        def _():
            up(i).wait_recv()
            when(second_up_valid, lambda: second_up(i).start())
            to_sibling(i, 2).start()

        @pl.when(chip >= 3)
        def _():
            down(i).wait_recv()
            when(second_down_valid, lambda: second_down(i).start())
            to_sibling(i, 6).start()

    def relay_second(i):
        @pl.when(chip >= 2)
        def _():
            second_up(i).wait_recv()
            to_sibling(i, 4).start()

    def sibling_arrivals(first, last):
        def arrivals(i, carry):
            for lane in range(4):
                @pl.when(s >= 2 * lane + 1)
                def _():
                    rows = slot_rows(2 * lane + 1, i)
                    remote(kv.at[rows], kv.at[rows], pair_send.at[lane, i], pair_recv.at[lane, i], at_seq(sibling)).wait_recv()
            return carry

        lax.fori_loop(first, last, arrivals, 0)

    query_row = lax.rem(lax.broadcasted_iota(jnp.int32, (2 * TILE, TILE), 0), TILE)
    key_row = lax.broadcasted_iota(jnp.int32, (2 * TILE, TILE), 1)

    def attend(u, phase):
        group = lax.div(u, 2)
        tile = lax.rem(u, 2)
        key_columns = aligned(group * HD, HD)
        value_columns = aligned(2 * HD + group * HD, HD)
        query = q[pl.ds(2 * group, 2), aligned(tile * TILE, TILE)].reshape(2 * TILE, HD)

        def block(slot, mask):
            rows = aligned((SLOTS - 1 - slot) * ROWS + phase * TILE, TILE)
            scores = lax.dot_general(
                query, kv[rows, key_columns], (((1,), (1,)), ((), ())), preferred_element_type=F32
            )
            weights = jnp.exp2(EXP_SCALE * jnp.tanh(scores * SCORE_SCALE))
            if mask is not None:
                weights = jnp.where(mask, weights, 0.0)
            product = jnp.dot(weights.astype(BF16), kv[rows, value_columns], preferred_element_type=F32)
            return weights[:, :128] + weights[:, 128:], product

        def add(parts):
            partial, product = parts[0]
            for more_partial, more_product in parts[1:]:
                partial = partial + more_partial
                product = product + more_product
            den[u] += partial
            acc[u] += product

        if phase == 0:
            partial, product = block(0, key_row <= tile * TILE + query_row)
            den[u] = partial
            acc[u] = product

            @pl.when((tile == 0) & (s >= 8))
            def _():
                add([block(8, key_row > query_row)])
        else:
            @pl.when(tile == 1)
            def _():
                add([block(0, key_row <= query_row)])

            @pl.when(s >= 8)
            def _():
                add([block(8, TILE + key_row > tile * TILE + query_row)])

        count = jnp.minimum(7, s)
        groups = lax.div(count, 3)

        def triple(j, carry):
            add([block(1 + 3 * j + k, None) for k in range(3)])
            return carry

        def single(j, carry):
            add([block(1 + 3 * groups + j, None)])
            return carry

        lax.fori_loop(0, groups, triple, 0)
        lax.fori_loop(0, count - 3 * groups, single, 0)

    def step(t, carry):
        lag = 1 + ((z == 1) & (x == 0)).astype(jnp.int32)

        when(t < CHUNKS, lambda: own(t))
        when((t >= 1) & (t < CHUNKS + 1), lambda: relay_onward(t - 1))
        when((t >= lag) & (t < CHUNKS + lag), lambda: relay_far(t - lag))
        when((t >= lag + 1) & (t < CHUNKS + lag + 1), lambda: relay_near(t - lag - 1))
        when((t >= lag + 2) & (t < CHUNKS + lag + 2), lambda: relay_second(t - lag - 2))

        @pl.when(t == 0)
        def _():
            for k in range(3):
                weight_along_y(k).wait_recv()
            for k in range(3):
                weight_along_x(k).start()

        @pl.when(t == 3)
        def _():
            for k in range(3):
                weight_along_x(k).wait_recv()
            weight_sibling().start()

        @pl.when(t == CHUNKS - 1)
        def _():
            sibling_arrivals(0, CHUNKS // 2)

        when((t >= CHUNKS - 1) & (t < CHUNKS - 1 + UNITS), lambda: attend(t - CHUNKS + 1, 0))
        return carry

    lax.fori_loop(0, CHUNKS + 4, step, 0)
    sibling_arrivals(CHUNKS // 2, CHUNKS)
    weight_sibling().wait_recv()
    loads[4].wait()

    def unit_exchange(u):
        return remote(att.at[head, u], att.at[head, u], att_send.at[u], att_recv.at[u], partner)

    def unit_arrival(u):
        return remote(att.at[head, u], att.at[other, u], att_send.at[u], att_recv.at[u], partner)

    def project(u, which, fresh):
        group = lax.div(u, 2)
        tile = lax.rem(u, 2)
        rows = aligned(tile * TILE, TILE)

        def columns_of(j, carry):
            columns = aligned(j * 256, 256)
            product = jnp.dot(
                att[which, u], wob[aligned(which * 1024 + group * 512, 512), columns], preferred_element_type=F32
            )

            @pl.when(fresh)
            def _():
                branch[rows, columns] = product

            @pl.when(jnp.logical_not(fresh))
            def _():
                branch[rows, columns] += product

            return carry

        lax.fori_loop(0, HALF // 256, columns_of, 0)

    def second_phase(u, carry):
        attend(u, 1)
        denominator = jnp.sum(den[u], axis=-1, keepdims=True)
        attended = (acc[u] / denominator).astype(BF16)
        att[head, u] = jnp.concatenate([attended[:TILE], attended[TILE:]], axis=1)
        unit_exchange(u).start()
        project(u, head, u < 2)
        return carry

    lax.fori_loop(0, UNITS, second_phase, 0)

    diagonal = lax.broadcasted_iota(jnp.int32, (128, 128), 0) == lax.broadcasted_iota(jnp.int32, (128, 128), 1)

    def sums_copy(tile):
        return remote(sums.at[0, tile], sums.at[1, tile], sum_send.at[tile], sum_recv.at[tile], partner)

    def send_sums(tile):
        share = branch[aligned(tile * TILE, TILE)]
        totals = jnp.sum(share * share, axis=-1, keepdims=True)
        for block in range(2):
            spread = jnp.where(diagonal, totals[block * 128 : (block + 1) * 128], 0.0)
            sums[0, tile, block * 8 : (block + 1) * 8] = jnp.broadcast_to(jnp.sum(spread, axis=0, keepdims=True), (8, 128))
        sums_copy(tile).start()

    def output_copy(tile):
        rows = aligned(tile * TILE, TILE)
        return pltpu.make_async_copy(obuf.at[rows], out.at[rows], out_sem.at[tile])

    def finish(tile):
        sums_copy(tile).wait_recv()
        for block in range(2):
            rows = aligned(tile * TILE + block * 128, 128)
            both = sums[0, tile, block * 8 : block * 8 + 1] + sums[1, tile, block * 8 : block * 8 + 1]
            squares = jnp.sum(jnp.where(diagonal, both, 0.0), axis=1, keepdims=True)
            inverse = lax.rsqrt(squares / D + norm_epsilon)
            obuf[rows] = (xbuf[head, rows].astype(F32) + post[...] * branch[rows] * inverse).astype(BF16)
        output_copy(tile).start()

    def third_phase(u, carry):
        unit_arrival(u).wait_recv()
        project(u, other, u < 0)
        when(u >= 2, lambda: send_sums(u - 2))
        return carry

    lax.fori_loop(0, UNITS, third_phase, 0)
    finish(0)
    finish(1)

    def drain(i, carry):
        token_copy(i).wait_send()
        when(far_direct(i), lambda: far(i).wait_send())
        when(far_by_transit(i), lambda: far_transit(i).wait_send())
        when(onward_here(i), lambda: onward(i).wait_send())
        when(up_own | up_relay, lambda: up(i).wait_send())
        when(down_own | down_relay, lambda: down(i).wait_send())
        when(second_up_valid, lambda: second_up(i).wait_send())
        when(second_down_valid, lambda: second_down(i).wait_send())
        for slot in (0, 2, 4, 6, 8):
            sends = (slot <= s) & ((core == 0) if slot == 0 else (core == 1) if slot == 8 else (core >= 0))
            when(sends, lambda: to_sibling(i, slot).wait_send())
        return carry

    lax.fori_loop(0, CHUNKS, drain, 0)
    weight_slice().wait_send()
    for k in range(3):
        weight_along_y(k).wait_send()
        weight_along_x(k).wait_send()
    weight_sibling().wait_send()
    for u in range(UNITS):
        unit_exchange(u).wait_send()
    for tile in range(2):
        sums_copy(tile).wait_send()
        output_copy(tile).wait()


def local(tokens, pre_gain, query_weight, key_weight, value_weight, out_weight, post_gain):
    cosine, sine = rope_tables(ROWS)
    vmem = pl.BlockSpec(memory_space=pltpu.VMEM)
    hbm = pl.BlockSpec(memory_space=pl.ANY)
    dma = pltpu.SemaphoreType.DMA
    return pl.pallas_call(
        layer_kernel,
        out_shape=jax.ShapeDtypeStruct((ROWS, HALF), BF16),
        in_specs=[hbm, vmem, hbm, hbm, hbm, hbm, vmem, vmem, vmem],
        out_specs=hbm,
        scratch_shapes=[
            pltpu.VMEM((2, ROWS, HALF), BF16),
            pltpu.VMEM((PART, D), BF16),
            pltpu.VMEM((D, 4 * HD), BF16),
            pltpu.VMEM((D, 2 * HD), BF16),
            pltpu.VMEM((D, 2 * HD), BF16),
            pltpu.VMEM((2048, HALF), BF16),
            pltpu.VMEM((4, ROWS, HD), BF16),
            pltpu.VMEM((SLOTS * ROWS, 4 * HD), BF16),
            pltpu.VMEM((UNITS, 2 * TILE, HD), F32),
            pltpu.VMEM((UNITS, 2 * TILE, 128), F32),
            pltpu.VMEM((2, UNITS, TILE, 2 * HD), BF16),
            pltpu.VMEM((ROWS, HALF), F32),
            pltpu.VMEM((2, PART, 4 * HD), BF16),
            pltpu.VMEM((2, 2, 16, 128), F32),
            pltpu.VMEM((ROWS, HALF), BF16),
            dma((5,)),
            dma((CHUNKS,)),
            dma((CHUNKS,)),
            dma((5, CHUNKS)),
            dma((4, CHUNKS)),
            dma((4, CHUNKS)),
            dma((4, CHUNKS)),
            dma((CHUNKS,)),
            dma((2,)),
            dma((2,)),
            dma((8,)),
            dma((8,)),
            dma((UNITS,)),
            dma((UNITS,)),
            dma((2,)),
            dma((2,)),
            dma((2,)),
        ],
        compiler_params=pltpu.CompilerParams(
            collective_id=0, has_side_effects=True, vmem_limit_bytes=63 * 1024 * 1024
        ),
        name="layer",
    )(
        tokens, pre_gain[None, :], query_weight, key_weight, value_weight, out_weight,
        post_gain[None, :], cosine, sine,
    )


def solution(mesh):
    placed = (
        P("seq", "head"),
        P(),
        P(None, "head"),
        P(None, "head"),
        P(None, "head"),
        P("head", None),
        P("head"),
    )
    return jax.shard_map(
        local, mesh=mesh, in_specs=placed, out_specs=P("seq", "head"), check_vma=False
    )
```

time: 190 us -> 136 us (0.72)
  the two profiles are of different devices: /device:TPU:2 before, /device:TPU:64 now
where the time goes in v1:
time: 136 us
  Pallas kernels  129 us (95%)
  local copies, waits for them, and re-layouts  5.47 us (4%)
  other arithmetic  1.8 us (1%)
    pallas_call x1, Pallas kernels, local(): pl.pallas_call(layer_kernel, out_shape=jax.ShapeDtypeStruct((ROWS, HALF),...  129 us
    unnamed x1, local copies, waits for them, and re-layouts  2.85 us

profile of v1, /device:TPU:64, one launch (start us, length us, event | category | flops | bytes accessed | tf_op | source)
XLA Modules:
  0.0 136.1 jit_solution(16955724476144690304)
XLA Ops:
  0.0 1.3 broadcast_in_dim.9.post
  1.3 1.3 broadcast_in_dim.8.gain
  2.6 1.8 %multiply_sine_fusion = (f32[512,128]{1,0:T(8,128)}, f32[512,128]{1,0:T(8,128)}) fusion(f32[128]{0:T(128)S(1)} %multiply_exponential_fusion, f32[512]{0:T(512)S(1)} %add_convert_fusion), kind=kLoop, calls=%fused_computation | loop fusion | flops 65536 | bytes 526848 | tf_op jit(solution)/shard_map/sin | solution.py:33
  4.4 128.9 %layer.1 = bf16[512,1792]{1,0:T(8,128)(2,1)} custom-call(bf16[512,1792]{1,0:T(8,128)(2,1)} %tok.1, f32[1,3584]{1,0:T(1,128)} %broadcast_in_dim.8.gain, bf16[3584,1024]{1,0:T(8,128)(2,1)} %wq.1, bf16[3584,512]{1,0:T(8,128)(2,1)} %wk.1, bf16[3584,512]{1,0:T(8,128)(2,1)} %wv.1, bf16[1024,3584]{1,0:T(8,128)(2,1)} %wo.1, f32[1,1792]{1,0:T(1,128)} %broadcast_in_dim.9.post, ...), custom_call_target="tpu_custom_call" | custom-call | tf_op jit(solution)/shard_map/layer/pallas_call | solution.py:501
  133.3 2.8 %copy.9 = bf16[512,1792]{1,0:T(8,128)(2,1)} copy(bf16[512,1792]{1,0:T(8,128)(2,1)} %layer.1) | data formatting | bytes 3670016
  (2 shorter events, 0.0 us)

commit v2 on v1

--- a/solution.py
+++ b/solution.py
@@ -2,6 +2,7 @@
 
 import jax
 import jax.numpy as jnp
+import numpy as np
 from jax import lax
 from jax.experimental import pallas as pl
 from jax.experimental.pallas import tpu as pltpu
@@ -26,11 +27,11 @@
 SCORE_SCALE = HD ** (-0.5) / softcap_limit
 
 
-def rope_tables(row_count):
-    positions = lax.axis_index("seq") * row_count + jnp.arange(row_count, dtype=jnp.int32)
-    frequency = jnp.exp(-jnp.log(rope_base) * (2.0 * jnp.arange(HD // 2, dtype=F32) / HD))
-    angles = positions.astype(F32)[:, None] * frequency[None, :]
-    return jnp.cos(angles), jnp.sin(angles)
+def rope_rows():
+    frequency = rope_base ** (-2.0 * np.arange(HD // 2) / HD)
+    angles = np.arange(ROWS)[:, None] * frequency[None, :]
+    table = np.stack([np.cos(angles), np.sin(angles)])
+    return table.astype(np.float32), np.broadcast_to(frequency, (8, HD // 2)).astype(np.float32)
 
 
 def aligned(start, size, step=None):
@@ -46,8 +47,8 @@
 
 
 def layer_kernel(
-    tok, gain, wq, wk, wv, wo, post, cosine, sine, out,
-    xbuf, xn, wqb, wkb, wvb, wob, q, kv, acc, den, att, branch, transit, sums, obuf,
+    tok, gain, wq, wk, wv, wo, post, turns, frequency, out,
+    xbuf, xn, wqb, wkb, wvb, wob, q, kv, acc, den, att, branch, transit, sums, obuf, cosine, sine,
     load_sem, z_send, z_recv, send, recv, pair_send, pair_recv,
     transit_send, transit_recv, onward_send, w_send, w_recv, att_send, att_recv, sum_send, sum_recv, out_sem,
 ):
@@ -126,9 +127,10 @@
         rows = aligned(theirs + slice_index * 32, 32)
         return remote(wob.at[rows], wob.at[rows], w_send.at[1 + k], w_recv.at[1 + k], at_seq(ring_y[k]))
 
-    def weight_along_x(k):
-        rows = aligned(theirs + (core * 4 + x) * 128, 128)
-        return remote(wob.at[rows], wob.at[rows], w_send.at[4 + k], w_recv.at[4 + k], at_seq(ring_x[k]))
+    def weight_along_x(hop):
+        column = lax.rem(x + 1, 4) if hop == 1 else x
+        rows = aligned(theirs + (core * 4 + column) * 128, 128)
+        return remote(wob.at[rows], wob.at[rows], w_send.at[4 + hop], w_recv.at[4 + hop], at_seq(ring_x[0 if hop == 2 else 2]))
 
     def weight_sibling():
         rows = aligned(theirs + core * 512, 512)
@@ -151,7 +153,7 @@
         return flow(0, i, 0, 8, s + 8)
 
     def far_transit(i):
-        column = lax.rem(i, 4)
+        column = lax.rem(i + 1, 4)
         return remote(
             kv.at[slot_rows(0, i)], transit.at[lax.div(i, 4)], transit_send.at[i], transit_recv.at[lax.div(i, 4)],
             at_seq((16 + 4 * column + y) * 2 + core),
@@ -163,13 +165,13 @@
         )
 
     def far_direct(i):
-        return has_next & ((z == 1) | (x < 3) | (lax.rem(i, 4) == 0))
+        return has_next & ((z == 1) | (x < 3) | (lax.rem(i, 4) == 3))
 
     def far_by_transit(i):
-        return crosses & (lax.rem(i, 4) > 0)
+        return crosses & (lax.rem(i, 4) < 3)
 
     def onward_here(i):
-        return (z == 1) & (x > 0) & (lax.rem(i, 4) == x)
+        return (z == 1) & (x > 0) & (lax.rem(i, 4) == x - 1)
 
     def up(i):
         return flow(1, i, jnp.where(y < 3, 0, 8), 2, seq_up)
@@ -203,7 +205,13 @@
     weight_slice().start()
     for i in range(CHUNKS):
         token_copy(i).start()
-    for load in loads[:4]:
+    base = jnp.sum(jnp.where(lax.broadcasted_iota(jnp.int32, (8, HD // 2), 0) == 0, frequency[...], 0.0), axis=0, keepdims=True)
+    base = base * (s * ROWS).astype(F32)
+    base_cos = jnp.cos(base)
+    base_sin = jnp.sin(base)
+    cosine[...] = base_cos * turns[0] - base_sin * turns[1]
+    sine[...] = base_sin * turns[0] + base_cos * turns[1]
+    for load in loads[:3]:
         load.wait()
     weight_slice().wait_recv()
     for k in range(3):
@@ -223,23 +231,18 @@
         second = xbuf[1, rows].astype(F32)
         squares = jnp.sum(first * first, axis=-1, keepdims=True) + jnp.sum(second * second, axis=-1, keepdims=True)
         scale = lax.rsqrt(squares / D + norm_epsilon)
-        xn[:, :HALF] = (first * scale * gain[:, :HALF]).astype(BF16)
-        xn[:, HALF:] = (second * scale * gain[:, HALF:]).astype(BF16)
+        xn[rows, :HALF] = (first * scale * gain[:HALF][None, :]).astype(BF16)
+        xn[rows, HALF:] = (second * scale * gain[HALF:][None, :]).astype(BF16)
+
+        def value(j, carry):
+            product = jnp.dot(xn[rows], wvb[:, aligned(j * HD, HD)], preferred_element_type=F32)
+            kv[slot_rows(0, i), aligned(2 * HD + j * HD, HD)] = product.astype(BF16)
+            return carry
 
         def key(j, carry):
             columns = aligned(j * HD, HD)
-            product = jnp.dot(xn[...], wkb[:, columns], preferred_element_type=F32)
+            product = jnp.dot(xn[rows], wkb[:, columns], preferred_element_type=F32)
             kv[slot_rows(0, i), columns] = roped(product, rows)
-            return carry
-
-        def value(j, carry):
-            product = jnp.dot(xn[...], wvb[:, aligned(j * HD, HD)], preferred_element_type=F32)
-            kv[slot_rows(0, i), aligned(2 * HD + j * HD, HD)] = product.astype(BF16)
-            return carry
-
-        def query(j, carry):
-            product = jnp.dot(xn[...], wqb[:, aligned(j * HD, HD)], preferred_element_type=F32)
-            q[j, rows] = roped(product, rows)
             return carry
 
         lax.fori_loop(0, 2, value, 0)
@@ -249,6 +252,15 @@
         when(up_own, lambda: up(i).start())
         when(down_own, lambda: down(i).start())
         when(core == 0, lambda: to_sibling(i, 0).start())
+
+    def queries(tile):
+        rows = aligned(tile * TILE, TILE)
+
+        def query(j, carry):
+            product = jnp.dot(xn[rows], wqb[:, aligned(j * HD, HD)], preferred_element_type=F32)
+            q[j, rows] = roped(product, rows)
+            return carry
+
         lax.fori_loop(0, 4, query, 0)
 
     def relay_onward(i):
@@ -298,12 +310,11 @@
     query_row = lax.rem(lax.broadcasted_iota(jnp.int32, (2 * TILE, TILE), 0), TILE)
     key_row = lax.broadcasted_iota(jnp.int32, (2 * TILE, TILE), 1)
 
-    def attend(u, phase):
-        group = lax.div(u, 2)
-        tile = lax.rem(u, 2)
+    def attend(group, tile, phase):
+        u = 2 * tile + group
         key_columns = aligned(group * HD, HD)
         value_columns = aligned(2 * HD + group * HD, HD)
-        query = q[pl.ds(2 * group, 2), aligned(tile * TILE, TILE)].reshape(2 * TILE, HD)
+        query = q[pl.ds(2 * group, 2), tile * TILE : (tile + 1) * TILE].reshape(2 * TILE, HD)
 
         def block(slot, mask):
             rows = aligned((SLOTS - 1 - slot) * ROWS + phase * TILE, TILE)
@@ -316,77 +327,94 @@
             product = jnp.dot(weights.astype(BF16), kv[rows, value_columns], preferred_element_type=F32)
             return weights[:, :128] + weights[:, 128:], product
 
-        def add(parts):
+        def add(parts, fresh):
             partial, product = parts[0]
             for more_partial, more_product in parts[1:]:
                 partial = partial + more_partial
                 product = product + more_product
-            den[u] += partial
-            acc[u] += product
-
-        if phase == 0:
-            partial, product = block(0, key_row <= tile * TILE + query_row)
-            den[u] = partial
-            acc[u] = product
-
-            @pl.when((tile == 0) & (s >= 8))
-            def _():
-                add([block(8, key_row > query_row)])
-        else:
-            @pl.when(tile == 1)
-            def _():
-                add([block(0, key_row <= query_row)])
-
-            @pl.when(s >= 8)
-            def _():
-                add([block(8, TILE + key_row > tile * TILE + query_row)])
-
-        count = jnp.minimum(7, s)
-        groups = lax.div(count, 3)
-
-        def triple(j, carry):
-            add([block(1 + 3 * j + k, None) for k in range(3)])
-            return carry
-
-        def single(j, carry):
-            add([block(1 + 3 * groups + j, None)])
-            return carry
-
-        lax.fori_loop(0, groups, triple, 0)
-        lax.fori_loop(0, count - 3 * groups, single, 0)
+            if fresh:
+                den[u] = partial
+                acc[u] = product
+            else:
+                den[u] += partial
+                acc[u] += product
+
+        def causal():
+            return block(0, (key_row <= query_row) if tile == phase else None)
+
+        def edge():
+            return block(8, (key_row > query_row) if tile == phase else None)
+
+        has_causal = phase <= tile
+        has_edge = phase >= tile
+
+        @pl.when(s >= 8)
+        def _():
+            parts = [block(slot, None) for slot in range(1, 8)]
+            if has_causal:
+                parts.insert(0, causal())
+            if has_edge:
+                parts.append(edge())
+            add(parts, phase == 0)
+
+        @pl.when(s < 8)
+        def _():
+            if phase == 0:
+                add([causal()], True)
+            elif has_causal:
+                add([causal()], False)
+
+            def single(j, carry):
+                add([block(1 + j, None)], False)
+                return carry
+
+            lax.fori_loop(0, jnp.minimum(7, s), single, 0)
+
+    lag = 1 + ((z == 1) & (x == 0)).astype(jnp.int32)
+    first_attend = lag + 5
+
+    def relayed(t, hops):
+        return jnp.where(t >= CHUNKS + hops, CHUNKS, jnp.clip(t - lag + 1 - hops, 0, CHUNKS))
+
+    def relay(t, hops, action):
+        def one(i, carry):
+            action(i)
+            return carry
+
+        lax.fori_loop(relayed(t - 1, hops), relayed(t, hops), one, 0)
 
     def step(t, carry):
-        lag = 1 + ((z == 1) & (x == 0)).astype(jnp.int32)
-
         when(t < CHUNKS, lambda: own(t))
         when((t >= 1) & (t < CHUNKS + 1), lambda: relay_onward(t - 1))
-        when((t >= lag) & (t < CHUNKS + lag), lambda: relay_far(t - lag))
-        when((t >= lag + 1) & (t < CHUNKS + lag + 1), lambda: relay_near(t - lag - 1))
-        when((t >= lag + 2) & (t < CHUNKS + lag + 2), lambda: relay_second(t - lag - 2))
+        relay(t, 0, relay_far)
+        relay(t, 1, relay_near)
+        relay(t, 2, relay_second)
 
         @pl.when(t == 0)
         def _():
             for k in range(3):
                 weight_along_y(k).wait_recv()
-            for k in range(3):
-                weight_along_x(k).start()
-
-        @pl.when(t == 3)
-        def _():
-            for k in range(3):
-                weight_along_x(k).wait_recv()
-            weight_sibling().start()
-
-        @pl.when(t == CHUNKS - 1)
-        def _():
-            sibling_arrivals(0, CHUNKS // 2)
-
-        when((t >= CHUNKS - 1) & (t < CHUNKS - 1 + UNITS), lambda: attend(t - CHUNKS + 1, 0))
+            weight_along_x(0).start()
+            loads[3].wait()
+
+        @pl.when(t == 4)
+        def _():
+            weight_along_x(0).wait_recv()
+            weight_along_x(1).start()
+
+        when(t == CHUNKS, lambda: weight_along_x(2).start())
+        when(t == 3, lambda: queries(0))
+        when(t == CHUNKS - 1, lambda: queries(1))
+        when(t == first_attend, lambda: sibling_arrivals(0, CHUNKS // 2))
+        when((t >= first_attend) & (t < first_attend + 2), lambda: attend(t - first_attend, 0, 0))
+        when((t >= first_attend + 2) & (t < first_attend + 4), lambda: attend(t - first_attend - 2, 1, 0))
         return carry
 
-    lax.fori_loop(0, CHUNKS + 4, step, 0)
+    lax.fori_loop(0, CHUNKS + 3, step, 0)
+    for hop in (1, 2):
+        weight_along_x(hop).wait_recv()
+    weight_sibling().start()
     sibling_arrivals(CHUNKS // 2, CHUNKS)
-    weight_sibling().wait_recv()
     loads[4].wait()
 
     def unit_exchange(u):
@@ -395,39 +423,40 @@
     def unit_arrival(u):
         return remote(att.at[head, u], att.at[other, u], att_send.at[u], att_recv.at[u], partner)
 
-    def project(u, which, fresh):
-        group = lax.div(u, 2)
-        tile = lax.rem(u, 2)
-        rows = aligned(tile * TILE, TILE)
+    def project(tile, which, groups, fresh):
+        rows = slice(tile * TILE, (tile + 1) * TILE)
 
         def columns_of(j, carry):
-            columns = aligned(j * 256, 256)
-            product = jnp.dot(
-                att[which, u], wob[aligned(which * 1024 + group * 512, 512), columns], preferred_element_type=F32
-            )
-
-            @pl.when(fresh)
-            def _():
+            columns = aligned(j * 896, 896)
+            product = None
+            for group in groups:
+                term = jnp.dot(
+                    att[which, 2 * tile + group], wob[aligned(which * 1024 + group * 512, 512), columns],
+                    preferred_element_type=F32,
+                )
+                product = term if product is None else product + term
+            if fresh:
                 branch[rows, columns] = product
-
-            @pl.when(jnp.logical_not(fresh))
-            def _():
+            else:
                 branch[rows, columns] += product
-
-            return carry
-
-        lax.fori_loop(0, HALF // 256, columns_of, 0)
-
-    def second_phase(u, carry):
-        attend(u, 1)
-        denominator = jnp.sum(den[u], axis=-1, keepdims=True)
-        attended = (acc[u] / denominator).astype(BF16)
-        att[head, u] = jnp.concatenate([attended[:TILE], attended[TILE:]], axis=1)
-        unit_exchange(u).start()
-        project(u, head, u < 2)
-        return carry
-
-    lax.fori_loop(0, UNITS, second_phase, 0)
+            return carry
+
+        lax.fori_loop(0, HALF // 896, columns_of, 0)
+
+    for tile in range(2):
+        def second_phase(group, carry):
+            u = 2 * tile + group
+            attend(group, tile, 1)
+            denominator = jnp.sum(den[u], axis=-1, keepdims=True)
+            attended = (acc[u] / denominator).astype(BF16)
+            att[head, u] = jnp.concatenate([attended[:TILE], attended[TILE:]], axis=1)
+            unit_exchange(u).start()
+            return carry
+
+        lax.fori_loop(0, 2, second_phase, 0)
+        if tile == 1:
+            for part in range(2):
+                project(part, head, (0, 1), True)
 
     diagonal = lax.broadcasted_iota(jnp.int32, (128, 128), 0) == lax.broadcasted_iota(jnp.int32, (128, 128), 1)
 
@@ -453,17 +482,20 @@
             both = sums[0, tile, block * 8 : block * 8 + 1] + sums[1, tile, block * 8 : block * 8 + 1]
             squares = jnp.sum(jnp.where(diagonal, both, 0.0), axis=1, keepdims=True)
             inverse = lax.rsqrt(squares / D + norm_epsilon)
-            obuf[rows] = (xbuf[head, rows].astype(F32) + post[...] * branch[rows] * inverse).astype(BF16)
+            obuf[rows] = (xbuf[head, rows].astype(F32) + post[...][None, :] * branch[rows] * inverse).astype(BF16)
         output_copy(tile).start()
 
-    def third_phase(u, carry):
-        unit_arrival(u).wait_recv()
-        project(u, other, u < 0)
-        when(u >= 2, lambda: send_sums(u - 2))
-        return carry
-
-    lax.fori_loop(0, UNITS, third_phase, 0)
+    weight_sibling().wait_recv()
+    unit_arrival(0).wait_recv()
+    unit_arrival(1).wait_recv()
+    project(0, other, (0, 1), False)
+    send_sums(0)
+    unit_arrival(2).wait_recv()
+    project(1, other, (0,), False)
     finish(0)
+    unit_arrival(3).wait_recv()
+    project(1, other, (1,), False)
+    send_sums(1)
     finish(1)
 
     def drain(i, carry):
@@ -494,7 +526,7 @@
 
 
 def local(tokens, pre_gain, query_weight, key_weight, value_weight, out_weight, post_gain):
-    cosine, sine = rope_tables(ROWS)
+    turns, frequency = rope_rows()
     vmem = pl.BlockSpec(memory_space=pltpu.VMEM)
     hbm = pl.BlockSpec(memory_space=pl.ANY)
     dma = pltpu.SemaphoreType.DMA
@@ -505,7 +537,7 @@
         out_specs=hbm,
         scratch_shapes=[
             pltpu.VMEM((2, ROWS, HALF), BF16),
-            pltpu.VMEM((PART, D), BF16),
+            pltpu.VMEM((ROWS, D), BF16),
             pltpu.VMEM((D, 4 * HD), BF16),
             pltpu.VMEM((D, 2 * HD), BF16),
             pltpu.VMEM((D, 2 * HD), BF16),
@@ -519,6 +551,8 @@
             pltpu.VMEM((2, PART, 4 * HD), BF16),
             pltpu.VMEM((2, 2, 16, 128), F32),
             pltpu.VMEM((ROWS, HALF), BF16),
+            pltpu.VMEM((ROWS, HD // 2), F32),
+            pltpu.VMEM((ROWS, HD // 2), F32),
             dma((5,)),
             dma((CHUNKS,)),
             dma((CHUNKS,)),
@@ -542,8 +576,8 @@
         ),
         name="layer",
     )(
-        tokens, pre_gain[None, :], query_weight, key_weight, value_weight, out_weight,
-        post_gain[None, :], cosine, sine,
+        tokens, pre_gain, query_weight, key_weight, value_weight, out_weight,
+        post_gain, turns, frequency,
     )
 
 

time: 136 us -> 135 us (level)
  Pallas kernels: 129 us -> 132 us
  local copies, waits for them, and re-layouts: 5.47 us -> 2.85 us
  other arithmetic: 1.8 us -> 0 us
    pallas_call x1, Pallas kernels: 129 us -> 132 us  [local(): pl.pallas_call(layer_kernel, out_shape=jax.ShapeDtypeStruct((ROWS, HALF),...]
    broadcast_in_dim x2 -> x0, local copies, waits for them, and re-layouts: 2.62 us -> none  [the longest x1 1.32 us: local(): pre_gain[None, :]]
    sin x1 -> x0, other arithmetic: 1.79 us -> none  [rope_tables(): return (jnp.cos(angles), jnp.sin(angles))]
where the time goes in v2:
time: 135 us
  Pallas kernels  132 us (98%)
  local copies, waits for them, and re-layouts  2.85 us (2%)
    pallas_call x1, Pallas kernels, local(): pl.pallas_call(layer_kernel, out_shape=jax.ShapeDtypeStruct((ROWS, HALF),...  132 us
    unnamed x1, local copies, waits for them, and re-layouts  2.85 us

profile of v2, /device:TPU:64, one launch (start us, length us, event | category | flops | bytes accessed | tf_op | source)
XLA Modules:
  0.0 134.7 jit_solution(11646466574979994474)
XLA Ops:
  0.0 131.8 %layer.1 = bf16[512,1792]{1,0:T(8,128)(2,1)} custom-call(bf16[512,1792]{1,0:T(8,128)(2,1)} %tok.1, f32[3584]{0:T(1024)} %gain.1, bf16[3584,1024]{1,0:T(8,128)(2,1)} %wq.1, bf16[3584,512]{1,0:T(8,128)(2,1)} %wk.1, bf16[3584,512]{1,0:T(8,128)(2,1)} %wv.1, bf16[1024,3584]{1,0:T(8,128)(2,1)} %wo.1, f32[1792]{0:T(1024)} %post.1, ...), custom_call_target="tpu_custom_call" | custom-call | tf_op jit(solution)/shard_map/layer/pallas_call | solution.py:533
  131.8 2.8 %copy.11 = bf16[512,1792]{1,0:T(8,128)(2,1)} copy(bf16[512,1792]{1,0:T(8,128)(2,1)} %layer.1) | data formatting | bytes 3670016

commit v3 on v2

--- a/solution.py
+++ b/solution.py
@@ -73,6 +73,7 @@
         return (target, head)
 
     partner = (s, other)
+    weight_partner = (s + 32 - 64 * z, other)
 
     def remote(source, target, send_sem, recv_sem, device):
         return pltpu.make_async_remote_copy(
@@ -98,20 +99,21 @@
         pl.semaphore_signal(barrier, inc=1, device_id=device, device_id_type=MESH)
 
     greet(partner)
+    greet(weight_partner)
     greet(at_seq(sibling))
     for target in ring_y + ring_x:
         greet(at_seq(target))
 
-    @pl.when(z == 1)
+    @pl.when((z == 1) & (x < 3))
     def _():
         greet(at_seq((12 + y) * 2 + core))
 
     @pl.when(crosses)
     def _():
-        for column in range(4):
+        for column in range(3):
             greet(at_seq((16 + 4 * column + y) * 2 + core))
 
-    pl.semaphore_wait(barrier, 8 + z + 4 * crosses.astype(jnp.int32))
+    pl.semaphore_wait(barrier, 9 + ((z == 1) & (x < 3)).astype(jnp.int32) + 3 * crosses.astype(jnp.int32))
 
     slice_index = (core * 4 + x) * 4 + y
     mine = head * 1024
@@ -120,7 +122,7 @@
     def weight_slice():
         return remote(
             wo.at[aligned(slice_index * 32, 32), other_columns], wob.at[aligned(mine + slice_index * 32, 32)],
-            w_send.at[0], w_recv.at[0], partner,
+            w_send.at[0], w_recv.at[0], weight_partner,
         )
 
     def weight_along_y(k):
@@ -153,25 +155,25 @@
         return flow(0, i, 0, 8, s + 8)
 
     def far_transit(i):
-        column = lax.rem(i + 1, 4)
+        column = lax.rem(i + 2, 3)
         return remote(
-            kv.at[slot_rows(0, i)], transit.at[lax.div(i, 4)], transit_send.at[i], transit_recv.at[lax.div(i, 4)],
+            kv.at[slot_rows(0, i)], transit.at[lax.div(i, 3)], transit_send.at[i], transit_recv.at[lax.div(i, 3)],
             at_seq((16 + 4 * column + y) * 2 + core),
         )
 
     def onward(i):
         return remote(
-            transit.at[lax.div(i, 4)], kv.at[slot_rows(8, i)], onward_send.at[lax.div(i, 4)], recv.at[0, i], at_seq(s - 8 * x)
+            transit.at[lax.div(i, 3)], kv.at[slot_rows(8, i)], onward_send.at[lax.div(i, 3)], recv.at[0, i], at_seq(s - 8 * x)
         )
 
     def far_direct(i):
-        return has_next & ((z == 1) | (x < 3) | (lax.rem(i, 4) == 3))
+        return has_next & ((z == 1) | (x < 3) | (lax.rem(i, 3) == 1))
 
     def far_by_transit(i):
-        return crosses & (lax.rem(i, 4) < 3)
+        return crosses & (lax.rem(i, 3) != 1)
 
     def onward_here(i):
-        return (z == 1) & (x > 0) & (lax.rem(i, 4) == x - 1)
+        return (z == 1) & (x > 0) & (lax.rem(i + 2, 3) == x)
 
     def up(i):
         return flow(1, i, jnp.where(y < 3, 0, 8), 2, seq_up)
@@ -397,12 +399,12 @@
             weight_along_x(0).start()
             loads[3].wait()
 
-        @pl.when(t == 4)
+        @pl.when(t == CHUNKS)
         def _():
             weight_along_x(0).wait_recv()
             weight_along_x(1).start()
-
-        when(t == CHUNKS, lambda: weight_along_x(2).start())
+            weight_along_x(2).start()
+
         when(t == 3, lambda: queries(0))
         when(t == CHUNKS - 1, lambda: queries(1))
         when(t == first_attend, lambda: sibling_arrivals(0, CHUNKS // 2))
@@ -411,9 +413,6 @@
         return carry
 
     lax.fori_loop(0, CHUNKS + 3, step, 0)
-    for hop in (1, 2):
-        weight_along_x(hop).wait_recv()
-    weight_sibling().start()
     sibling_arrivals(CHUNKS // 2, CHUNKS)
     loads[4].wait()
 
@@ -455,6 +454,9 @@
 
         lax.fori_loop(0, 2, second_phase, 0)
         if tile == 1:
+            for hop in (1, 2):
+                weight_along_x(hop).wait_recv()
+            weight_sibling().start()
             for part in range(2):
                 project(part, head, (0, 1), True)
 
@@ -492,10 +494,10 @@
     send_sums(0)
     unit_arrival(2).wait_recv()
     project(1, other, (0,), False)
-    finish(0)
     unit_arrival(3).wait_recv()
     project(1, other, (1,), False)
     send_sums(1)
+    finish(0)
     finish(1)
 
     def drain(i, carry):
@@ -548,7 +550,7 @@
             pltpu.VMEM((UNITS, 2 * TILE, 128), F32),
             pltpu.VMEM((2, UNITS, TILE, 2 * HD), BF16),
             pltpu.VMEM((ROWS, HALF), F32),
-            pltpu.VMEM((2, PART, 4 * HD), BF16),
+            pltpu.VMEM((3, PART, 4 * HD), BF16),
             pltpu.VMEM((2, 2, 16, 128), F32),
             pltpu.VMEM((ROWS, HALF), BF16),
             pltpu.VMEM((ROWS, HD // 2), F32),
@@ -561,8 +563,8 @@
             dma((4, CHUNKS)),
             dma((4, CHUNKS)),
             dma((CHUNKS,)),
-            dma((2,)),
-            dma((2,)),
+            dma((3,)),
+            dma((3,)),
             dma((8,)),
             dma((8,)),
             dma((UNITS,)),

time: 135 us -> 118 us (0.87)
  Pallas kernels: 132 us -> 115 us
    pallas_call x1, Pallas kernels: 132 us -> 115 us  [local(): pl.pallas_call(layer_kernel, out_shape=jax.ShapeDtypeStruct((ROWS, HALF),...]
where the time goes in v3:
time: 118 us
  Pallas kernels  115 us (97%)
  local copies, waits for them, and re-layouts  2.85 us (2%)
    pallas_call x1, Pallas kernels, local(): pl.pallas_call(layer_kernel, out_shape=jax.ShapeDtypeStruct((ROWS, HALF),...  115 us
    unnamed x1, local copies, waits for them, and re-layouts  2.85 us

profile of v3, /device:TPU:64, one launch (start us, length us, event | category | flops | bytes accessed | tf_op | source)
XLA Modules:
  0.0 117.6 jit_solution(18209601796367711929)
XLA Ops:
  0.0 114.7 %layer.1 = bf16[512,1792]{1,0:T(8,128)(2,1)} custom-call(bf16[512,1792]{1,0:T(8,128)(2,1)} %tok.1, f32[3584]{0:T(1024)} %gain.1, bf16[3584,1024]{1,0:T(8,128)(2,1)} %wq.1, bf16[3584,512]{1,0:T(8,128)(2,1)} %wk.1, bf16[3584,512]{1,0:T(8,128)(2,1)} %wv.1, bf16[1024,3584]{1,0:T(8,128)(2,1)} %wo.1, f32[1792]{0:T(1024)} %post.1, ...), custom_call_target="tpu_custom_call" | custom-call | tf_op jit(solution)/shard_map/layer/pallas_call | solution.py:535
  114.7 2.8 %copy.11 = bf16[512,1792]{1,0:T(8,128)(2,1)} copy(bf16[512,1792]{1,0:T(8,128)(2,1)} %layer.1) | data formatting | bytes 3670016

commit v4 on v3

--- a/solution.py
+++ b/solution.py
@@ -12,8 +12,10 @@
 HALF = 1792
 HD = 256
 ROWS = 512
-CHUNKS = 8
-PART = ROWS // CHUNKS
+PART = 64
+LONG = 7
+CHUNKS = 9
+HALF_READY = 4
 SLOTS = 9
 TILE = 256
 UNITS = 4
@@ -38,8 +40,26 @@
     return pl.ds(pl.multiple_of(start, step or size), size)
 
 
+def chunk_rows(chunk, offset=0):
+    index, size = chunk
+    start = index * PART if size == PART else LONG * PART + (index - LONG) * size
+    return aligned(offset + start, size)
+
+
 def slot_rows(slot, chunk):
-    return aligned((SLOTS - 1 - slot) * ROWS + chunk * PART, PART)
+    return chunk_rows(chunk, (SLOTS - 1 - slot) * ROWS)
+
+
+def each_chunk(first, last, action):
+    def over(low, high, size):
+        def one(i, carry):
+            action((i, size))
+            return carry
+
+        lax.fori_loop(low, high, one, 0)
+
+    over(first, jnp.minimum(last, LONG), PART)
+    over(jnp.maximum(first, LONG), last, PART // 2)
 
 
 def when(condition, action):
@@ -50,7 +70,7 @@
     tok, gain, wq, wk, wv, wo, post, turns, frequency, out,
     xbuf, xn, wqb, wkb, wvb, wob, q, kv, acc, den, att, branch, transit, sums, obuf, cosine, sine,
     load_sem, z_send, z_recv, send, recv, pair_send, pair_recv,
-    transit_send, transit_recv, onward_send, w_send, w_recv, att_send, att_recv, sum_send, sum_recv, out_sem,
+    transit_send, transit_recv, onward_send, across_send, w_send, w_recv, att_send, att_recv, sum_send, sum_recv, out_sem,
 ):
     s = lax.axis_index("seq")
     head = lax.axis_index("head")
@@ -104,16 +124,22 @@
     for target in ring_y + ring_x:
         greet(at_seq(target))
 
-    @pl.when((z == 1) & (x < 3))
+    @pl.when(z == 1)
     def _():
         greet(at_seq((12 + y) * 2 + core))
 
     @pl.when(crosses)
     def _():
-        for column in range(3):
+        for column in range(4):
             greet(at_seq((16 + 4 * column + y) * 2 + core))
 
-    pl.semaphore_wait(barrier, 9 + ((z == 1) & (x < 3)).astype(jnp.int32) + 3 * crosses.astype(jnp.int32))
+    crossing_pair = (crosses & (y >= 2)) | ((z == 1) & (x == 0) & (y < 2))
+
+    @pl.when(crossing_pair)
+    def _():
+        greet(at_seq((14 + y) * 2 + core))
+
+    pl.semaphore_wait(barrier, 9 + z + 4 * crosses.astype(jnp.int32) + crossing_pair.astype(jnp.int32))
 
     slice_index = (core * 4 + x) * 4 + y
     mine = head * 1024
@@ -138,62 +164,78 @@
         rows = aligned(theirs + core * 512, 512)
         return remote(wob.at[rows], wob.at[rows], w_send.at[7], w_recv.at[7], at_seq(sibling))
 
-    def token_copy(i):
-        rows = aligned(i * PART, PART)
-        return remote(tok.at[rows], xbuf.at[head, rows], z_send.at[i], z_recv.at[i], partner)
-
-    def token_arrival(i):
-        rows = aligned(i * PART, PART)
-        return remote(tok.at[rows], xbuf.at[other, rows], z_send.at[i], z_recv.at[i], partner)
-
-    def flow(index, i, source, slot, target):
+    def token_copy(c):
+        rows = chunk_rows(c)
+        return remote(tok.at[rows], xbuf.at[head, rows], z_send.at[c[0]], z_recv.at[c[0]], partner)
+
+    def token_arrival(c):
+        rows = chunk_rows(c)
+        return remote(tok.at[rows], xbuf.at[other, rows], z_send.at[c[0]], z_recv.at[c[0]], partner)
+
+    def flow(index, c, source, slot, target):
         return remote(
-            kv.at[slot_rows(source, i)], kv.at[slot_rows(slot, i)], send.at[index, i], recv.at[index, i], at_seq(target)
-        )
-
-    def far(i):
-        return flow(0, i, 0, 8, s + 8)
-
-    def far_transit(i):
-        column = lax.rem(i + 2, 3)
+            kv.at[slot_rows(source, c)], kv.at[slot_rows(slot, c)], send.at[index, c[0]], recv.at[index, c[0]],
+            at_seq(target),
+        )
+
+    def far(c):
+        return flow(0, c, 0, 8, s + 8)
+
+    def transit_slot(c):
+        return transit.at[lax.div(c[0], 3), pl.ds(0, c[1])]
+
+    def far_transit(c):
+        column = column_of(c)
         return remote(
-            kv.at[slot_rows(0, i)], transit.at[lax.div(i, 3)], transit_send.at[i], transit_recv.at[lax.div(i, 3)],
+            kv.at[slot_rows(0, c)], transit_slot(c), transit_send.at[c[0]], transit_recv.at[lax.div(c[0], 3)],
             at_seq((16 + 4 * column + y) * 2 + core),
         )
 
-    def onward(i):
+    def onward(c):
         return remote(
-            transit.at[lax.div(i, 3)], kv.at[slot_rows(8, i)], onward_send.at[lax.div(i, 3)], recv.at[0, i], at_seq(s - 8 * x)
-        )
-
-    def far_direct(i):
-        return has_next & ((z == 1) | (x < 3) | (lax.rem(i, 3) == 1))
-
-    def far_by_transit(i):
-        return crosses & (lax.rem(i, 3) != 1)
-
-    def onward_here(i):
-        return (z == 1) & (x > 0) & (lax.rem(i + 2, 3) == x)
-
-    def up(i):
-        return flow(1, i, jnp.where(y < 3, 0, 8), 2, seq_up)
-
-    def down(i):
-        return flow(2, i, jnp.where(y == 0, 0, 8), 6, seq_down)
-
-    def second_up(i):
-        return flow(3, i, 2, 4, seq_up)
-
-    def second_down(i):
+            transit_slot(c), kv.at[slot_rows(8, c)], onward_send.at[lax.div(c[0], 3)], recv.at[0, c[0]], at_seq(s - 8 * x)
+        )
+
+    def column_of(c):
+        return jnp.where(c[0] < LONG - 1, lax.rem(c[0], 3), jnp.where(c[0] == LONG - 1, 1, 0))
+
+    def in_own_column(c):
+        return column_of(c) == 0
+
+    def far_direct(c):
+        return has_next & ((z == 1) | (x < 3) | in_own_column(c))
+
+    def far_by_transit(c):
+        return crosses & jnp.logical_not(in_own_column(c))
+
+    def onward_here(c):
+        return (z == 1) & (x > 0) & (column_of(c) == x)
+
+    def across(c):
         return remote(
-            kv.at[slot_rows(6, i)], kv.at[slot_rows(4, i)], send.at[4, i], recv.at[3, i], at_seq(seq_down)
-        )
-
-    def to_sibling(i, slot):
+            kv.at[slot_rows(0, c)], kv.at[slot_rows(4, c)], across_send.at[c[0] - LONG], recv.at[3, c[0]],
+            at_seq((14 + y) * 2 + core),
+        )
+
+    def up(c):
+        return flow(1, c, jnp.where(y < 3, 0, 8), 2, seq_up)
+
+    def down(c):
+        return flow(2, c, jnp.where(y == 0, 0, 8), 6, seq_down)
+
+    def second_up(c):
+        return flow(3, c, 2, 4, seq_up)
+
+    def second_down(c):
+        return remote(
+            kv.at[slot_rows(6, c)], kv.at[slot_rows(4, c)], send.at[4, c[0]], recv.at[3, c[0]], at_seq(seq_down)
+        )
+
+    def to_sibling(c, slot):
         target = slot + 1 - 2 * core
         lane = lax.div(target - 1, 2)
         return remote(
-            kv.at[slot_rows(slot, i)], kv.at[slot_rows(target, i)], pair_send.at[lane, i], pair_recv.at[lane, i],
+            kv.at[slot_rows(slot, c)], kv.at[slot_rows(target, c)], pair_send.at[lane, c[0]], pair_recv.at[lane, c[0]],
             at_seq(sibling),
         )
 
@@ -201,12 +243,20 @@
     up_relay = (y == 3) & has_prev
     down_own = y == 0
     down_relay = (y > 0) & has_prev
-    second_up_valid = (y < 3) & (chip >= 1)
-    second_down_valid = (y == 1) & has_prev
+    crossed = (z == 1) & (x == 0)
+    goes_across = crosses & (y >= 2)
+
+    def second_up_valid(c):
+        valid = (y < 3) & (chip >= 1)
+        return valid if c[1] == PART else valid & jnp.logical_not(crossed & (y == 0))
+
+    def second_down_valid(c):
+        valid = (y == 1) & has_prev
+        return valid if c[1] == PART else valid & jnp.logical_not(crossed)
+
 
     weight_slice().start()
-    for i in range(CHUNKS):
-        token_copy(i).start()
+    each_chunk(0, CHUNKS, lambda c: token_copy(c).start())
     base = jnp.sum(jnp.where(lax.broadcasted_iota(jnp.int32, (8, HD // 2), 0) == 0, frequency[...], 0.0), axis=0, keepdims=True)
     base = base * (s * ROWS).astype(F32)
     base_cos = jnp.cos(base)
@@ -226,9 +276,9 @@
         trailing = values[:, HD // 2 :]
         return jnp.concatenate([leading * cos - trailing * sin, trailing * cos + leading * sin], axis=1).astype(BF16)
 
-    def own(i):
-        token_arrival(i).wait_recv()
-        rows = aligned(i * PART, PART)
+    def own(c):
+        token_arrival(c).wait_recv()
+        rows = chunk_rows(c)
         first = xbuf[0, rows].astype(F32)
         second = xbuf[1, rows].astype(F32)
         squares = jnp.sum(first * first, axis=-1, keepdims=True) + jnp.sum(second * second, axis=-1, keepdims=True)
@@ -238,22 +288,24 @@
 
         def value(j, carry):
             product = jnp.dot(xn[rows], wvb[:, aligned(j * HD, HD)], preferred_element_type=F32)
-            kv[slot_rows(0, i), aligned(2 * HD + j * HD, HD)] = product.astype(BF16)
+            kv[slot_rows(0, c), aligned(2 * HD + j * HD, HD)] = product.astype(BF16)
             return carry
 
         def key(j, carry):
             columns = aligned(j * HD, HD)
             product = jnp.dot(xn[rows], wkb[:, columns], preferred_element_type=F32)
-            kv[slot_rows(0, i), columns] = roped(product, rows)
+            kv[slot_rows(0, c), columns] = roped(product, rows)
             return carry
 
         lax.fori_loop(0, 2, value, 0)
         lax.fori_loop(0, 2, key, 0)
-        when(far_direct(i), lambda: far(i).start())
-        when(far_by_transit(i), lambda: far_transit(i).start())
-        when(up_own, lambda: up(i).start())
-        when(down_own, lambda: down(i).start())
-        when(core == 0, lambda: to_sibling(i, 0).start())
+        when(far_direct(c), lambda: far(c).start())
+        when(far_by_transit(c), lambda: far_transit(c).start())
+        if c[1] < PART:
+            when(goes_across, lambda: across(c).start())
+        when(up_own, lambda: up(c).start())
+        when(down_own, lambda: down(c).start())
+        when(core == 0, lambda: to_sibling(c, 0).start())
 
     def queries(tile):
         rows = aligned(tile * TILE, TILE)
@@ -265,49 +317,51 @@
 
         lax.fori_loop(0, 4, query, 0)
 
-    def relay_onward(i):
-        @pl.when(onward_here(i))
-        def _():
-            far_transit(i).wait_recv()
-            onward(i).start()
-
-    def relay_far(i):
+    def relay_onward(c):
+        @pl.when(onward_here(c))
+        def _():
+            far_transit(c).wait_recv()
+            onward(c).start()
+
+    def relay_far(c):
         @pl.when(has_prev)
         def _():
-            far(i).wait_recv()
-            when(up_relay, lambda: up(i).start())
-            when(down_relay, lambda: down(i).start())
-            when(core == 1, lambda: to_sibling(i, 8).start())
-
-    def relay_near(i):
+            far(c).wait_recv()
+            when(up_relay, lambda: up(c).start())
+            when(down_relay, lambda: down(c).start())
+            when(core == 1, lambda: to_sibling(c, 8).start())
+
+    def relay_up(c):
         @pl.when(chip >= 1)
         def _():
-            up(i).wait_recv()
-            when(second_up_valid, lambda: second_up(i).start())
-            to_sibling(i, 2).start()
-
+            up(c).wait_recv()
+            when(second_up_valid(c), lambda: second_up(c).start())
+            to_sibling(c, 2).start()
+
+    def relay_down(c):
         @pl.when(chip >= 3)
         def _():
-            down(i).wait_recv()
-            when(second_down_valid, lambda: second_down(i).start())
-            to_sibling(i, 6).start()
-
-    def relay_second(i):
+            down(c).wait_recv()
+            when(second_down_valid(c), lambda: second_down(c).start())
+            to_sibling(c, 6).start()
+
+    def relay_second(c):
         @pl.when(chip >= 2)
         def _():
-            second_up(i).wait_recv()
-            to_sibling(i, 4).start()
+            second_up(c).wait_recv()
+            to_sibling(c, 4).start()
 
     def sibling_arrivals(first, last):
-        def arrivals(i, carry):
+        def arrivals(c):
             for lane in range(4):
                 @pl.when(s >= 2 * lane + 1)
                 def _():
-                    rows = slot_rows(2 * lane + 1, i)
-                    remote(kv.at[rows], kv.at[rows], pair_send.at[lane, i], pair_recv.at[lane, i], at_seq(sibling)).wait_recv()
-            return carry
-
-        lax.fori_loop(first, last, arrivals, 0)
+                    rows = slot_rows(2 * lane + 1, c)
+                    remote(
+                        kv.at[rows], kv.at[rows], pair_send.at[lane, c[0]], pair_recv.at[lane, c[0]], at_seq(sibling)
+                    ).wait_recv()
+
+        each_chunk(first, last, arrivals)
 
     query_row = lax.rem(lax.broadcasted_iota(jnp.int32, (2 * TILE, TILE), 0), TILE)
     key_row = lax.broadcasted_iota(jnp.int32, (2 * TILE, TILE), 1)
@@ -372,32 +426,38 @@
 
             lax.fori_loop(0, jnp.minimum(7, s), single, 0)
 
-    lag = 1 + ((z == 1) & (x == 0)).astype(jnp.int32)
-    first_attend = lag + 5
-
-    def relayed(t, hops):
-        return jnp.where(t >= CHUNKS + hops, CHUNKS, jnp.clip(t - lag + 1 - hops, 0, CHUNKS))
-
-    def relay(t, hops, action):
-        def one(i, carry):
-            action(i)
-            return carry
-
-        lax.fori_loop(relayed(t - 1, hops), relayed(t, hops), one, 0)
+    late = crossed | crosses
+    far_lag = jnp.where(crossed, 2, 1)
+    near_lag = jnp.where(far_lag == 1, 2, far_lag + 1)
+    up_lag = jnp.where(y == 0, near_lag, 2)
+    down_lag = jnp.where(y == 3, 2, near_lag)
+    second_lag = jnp.where(y < 2, near_lag + 2, 4)
+    half_step = jnp.where(late, CHUNKS + 1, jnp.maximum(jnp.maximum(up_lag, down_lag), second_lag) + HALF_READY - 1)
+    half_units = jnp.where(late, 1, 2)
+
+    def relayed(t, lag, hops):
+        return jnp.where(
+            t >= CHUNKS + hops // 2, jnp.minimum(t - hops, CHUNKS), jnp.clip(t + 1 - lag, 0, CHUNKS)
+        )
+
+    def relay(t, lag, hops, action):
+        each_chunk(relayed(t - 1, lag, hops), relayed(t, lag, hops), action)
 
     def step(t, carry):
-        when(t < CHUNKS, lambda: own(t))
-        when((t >= 1) & (t < CHUNKS + 1), lambda: relay_onward(t - 1))
-        relay(t, 0, relay_far)
-        relay(t, 1, relay_near)
-        relay(t, 2, relay_second)
-
-        @pl.when(t == 0)
+        each_chunk(t, jnp.minimum(t + 1, CHUNKS), own)
+        each_chunk(jnp.maximum(t - 1, 0), jnp.minimum(t, CHUNKS), relay_onward)
+        relay(t, far_lag, 0, relay_far)
+        relay(t, up_lag, 1, relay_up)
+        relay(t, down_lag, 1, relay_down)
+        relay(t, second_lag, 2, relay_second)
+
+        @pl.when(t == 1)
         def _():
             for k in range(3):
                 weight_along_y(k).wait_recv()
             weight_along_x(0).start()
-            loads[3].wait()
+
+        when(t == 0, lambda: loads[3].wait())
 
         @pl.when(t == CHUNKS)
         def _():
@@ -406,14 +466,14 @@
             weight_along_x(2).start()
 
         when(t == 3, lambda: queries(0))
-        when(t == CHUNKS - 1, lambda: queries(1))
-        when(t == first_attend, lambda: sibling_arrivals(0, CHUNKS // 2))
-        when((t >= first_attend) & (t < first_attend + 2), lambda: attend(t - first_attend, 0, 0))
-        when((t >= first_attend + 2) & (t < first_attend + 4), lambda: attend(t - first_attend - 2, 1, 0))
+        when(t == half_step, lambda: sibling_arrivals(0, HALF_READY))
+        when((t >= half_step) & (t < half_step + half_units), lambda: attend(t - half_step, 0, 0))
+        when(t == 9, lambda: queries(1))
+        when((t == CHUNKS + 1) & jnp.logical_not(late), lambda: attend(0, 1, 0))
         return carry
 
     lax.fori_loop(0, CHUNKS + 3, step, 0)
-    sibling_arrivals(CHUNKS // 2, CHUNKS)
+    sibling_arrivals(HALF_READY, CHUNKS)
     loads[4].wait()
 
     def unit_exchange(u):
@@ -445,6 +505,8 @@
     for tile in range(2):
         def second_phase(group, carry):
             u = 2 * tile + group
+            if tile == 0:
+                when(late & (group == 1), lambda: attend(1, 0, 0))
             attend(group, tile, 1)
             denominator = jnp.sum(den[u], axis=-1, keepdims=True)
             attended = (acc[u] / denominator).astype(BF16)
@@ -453,12 +515,15 @@
             return carry
 
         lax.fori_loop(0, 2, second_phase, 0)
-        if tile == 1:
+        if tile == 0:
+            when(late, lambda: attend(0, 1, 0))
+            attend(1, 1, 0)
+        else:
+            project(0, head, (0, 1), True)
             for hop in (1, 2):
                 weight_along_x(hop).wait_recv()
             weight_sibling().start()
-            for part in range(2):
-                project(part, head, (0, 1), True)
+            project(1, head, (0, 1), True)
 
     diagonal = lax.broadcasted_iota(jnp.int32, (128, 128), 0) == lax.broadcasted_iota(jnp.int32, (128, 128), 1)
 
@@ -487,6 +552,21 @@
             obuf[rows] = (xbuf[head, rows].astype(F32) + post[...][None, :] * branch[rows] * inverse).astype(BF16)
         output_copy(tile).start()
 
+    def drain(c):
+        token_copy(c).wait_send()
+        when(far_direct(c), lambda: far(c).wait_send())
+        when(far_by_transit(c), lambda: far_transit(c).wait_send())
+        when(onward_here(c), lambda: onward(c).wait_send())
+        if c[1] < PART:
+            when(goes_across, lambda: across(c).wait_send())
+        when(up_own | up_relay, lambda: up(c).wait_send())
+        when(down_own | down_relay, lambda: down(c).wait_send())
+        when(second_up_valid(c), lambda: second_up(c).wait_send())
+        when(second_down_valid(c), lambda: second_down(c).wait_send())
+        for slot in (0, 2, 4, 6, 8):
+            sends = (slot <= s) & ((core == 0) if slot == 0 else (core == 1) if slot == 8 else (core >= 0))
+            when(sends, lambda: to_sibling(c, slot).wait_send())
+
     weight_sibling().wait_recv()
     unit_arrival(0).wait_recv()
     unit_arrival(1).wait_recv()
@@ -494,32 +574,18 @@
     send_sums(0)
     unit_arrival(2).wait_recv()
     project(1, other, (0,), False)
+    each_chunk(0, CHUNKS, drain)
+    weight_slice().wait_send()
+    for k in range(3):
+        weight_along_y(k).wait_send()
+        weight_along_x(k).wait_send()
+    weight_sibling().wait_send()
     unit_arrival(3).wait_recv()
     project(1, other, (1,), False)
     send_sums(1)
     finish(0)
     finish(1)
 
-    def drain(i, carry):
-        token_copy(i).wait_send()
-        when(far_direct(i), lambda: far(i).wait_send())
-        when(far_by_transit(i), lambda: far_transit(i).wait_send())
-        when(onward_here(i), lambda: onward(i).wait_send())
-        when(up_own | up_relay, lambda: up(i).wait_send())
-        when(down_own | down_relay, lambda: down(i).wait_send())
-        when(second_up_valid, lambda: second_up(i).wait_send())
-        when(second_down_valid, lambda: second_down(i).wait_send())
-        for slot in (0, 2, 4, 6, 8):
-            sends = (slot <= s) & ((core == 0) if slot == 0 else (core == 1) if slot == 8 else (core >= 0))
-            when(sends, lambda: to_sibling(i, slot).wait_send())
-        return carry
-
-    lax.fori_loop(0, CHUNKS, drain, 0)
-    weight_slice().wait_send()
-    for k in range(3):
-        weight_along_y(k).wait_send()
-        weight_along_x(k).wait_send()
-    weight_sibling().wait_send()
     for u in range(UNITS):
         unit_exchange(u).wait_send()
     for tile in range(2):
@@ -565,6 +631,7 @@
             dma((CHUNKS,)),
             dma((3,)),
             dma((3,)),
+            dma((2,)),
             dma((8,)),
             dma((8,)),
             dma((UNITS,)),

time: 118 us -> 113 us (0.958)
  Pallas kernels: 115 us -> 110 us
    pallas_call x1, Pallas kernels: 115 us -> 110 us  [local(): pl.pallas_call(layer_kernel, out_shape=jax.ShapeDtypeStruct((ROWS, HALF),...]
where the time goes in v4:
time: 113 us
  Pallas kernels  110 us (97%)
  local copies, waits for them, and re-layouts  2.85 us (3%)
    pallas_call x1, Pallas kernels, local(): pl.pallas_call(layer_kernel, out_shape=jax.ShapeDtypeStruct((ROWS, HALF),...  110 us
    unnamed x1, local copies, waits for them, and re-layouts  2.85 us

profile of v4, /device:TPU:64, one launch (start us, length us, event | category | flops | bytes accessed | tf_op | source)
XLA Modules:
  0.0 112.9 jit_solution(6601092167482324359)
XLA Ops:
  0.0 110.1 %layer.1 = bf16[512,1792]{1,0:T(8,128)(2,1)} custom-call(bf16[512,1792]{1,0:T(8,128)(2,1)} %tok.1, f32[3584]{0:T(1024)} %gain.1, bf16[3584,1024]{1,0:T(8,128)(2,1)} %wq.1, bf16[3584,512]{1,0:T(8,128)(2,1)} %wk.1, bf16[3584,512]{1,0:T(8,128)(2,1)} %wv.1, bf16[1024,3584]{1,0:T(8,128)(2,1)} %wo.1, f32[1792]{0:T(1024)} %post.1, ...), custom_call_target="tpu_custom_call" | custom-call | tf_op jit(solution)/shard_map/layer/pallas_call | solution.py:601
  110.1 2.8 %copy.11 = bf16[512,1792]{1,0:T(8,128)(2,1)} copy(bf16[512,1792]{1,0:T(8,128)(2,1)} %layer.1) | data formatting | bytes 3670016

commit v5 on v4

--- a/solution.py
+++ b/solution.py
@@ -133,13 +133,20 @@
         for column in range(4):
             greet(at_seq((16 + 4 * column + y) * 2 + core))
 
-    crossing_pair = (crosses & (y >= 2)) | ((z == 1) & (x == 0) & (y < 2))
-
-    @pl.when(crossing_pair)
+    @pl.when(crosses & (y >= 1))
+    def _():
+        greet(at_seq(jnp.where(y == 1, 16, 14 + y) * 2 + core))
+
+    @pl.when((z == 1) & (x == 0) & (y < 2))
     def _():
         greet(at_seq((14 + y) * 2 + core))
 
-    pl.semaphore_wait(barrier, 9 + z + 4 * crosses.astype(jnp.int32) + crossing_pair.astype(jnp.int32))
+    @pl.when((z == 1) & (x == 0) & (y == 0))
+    def _():
+        greet(at_seq(13 * 2 + core))
+
+    pairs_across = jnp.where(crosses, jnp.minimum(y, 1), jnp.where((z == 1) & (x == 0), jnp.maximum(2 - y, 0), 0))
+    pl.semaphore_wait(barrier, 9 + z + 4 * crosses.astype(jnp.int32) + pairs_across)
 
     slice_index = (core * 4 + x) * 4 + y
     mine = head * 1024
@@ -213,8 +220,8 @@
 
     def across(c):
         return remote(
-            kv.at[slot_rows(0, c)], kv.at[slot_rows(4, c)], across_send.at[c[0] - LONG], recv.at[3, c[0]],
-            at_seq((14 + y) * 2 + core),
+            kv.at[slot_rows(0, c)], kv.at[slot_rows(jnp.where(y == 1, 6, 4), c)], across_send.at[c[0] - LONG],
+            recv.at[jnp.where(y == 1, 2, 3), c[0]], at_seq(across_target),
         )
 
     def up(c):
@@ -242,9 +249,13 @@
     up_own = y < 3
     up_relay = (y == 3) & has_prev
     down_own = y == 0
-    down_relay = (y > 0) & has_prev
     crossed = (z == 1) & (x == 0)
-    goes_across = crosses & (y >= 2)
+    goes_across = crosses & (y >= 1)
+    across_target = jnp.where(y == 1, 16, 14 + y) * 2 + core
+
+    def down_valid(c):
+        relays = (y > 0) & has_prev
+        return down_own | (relays if c[1] == PART else relays & jnp.logical_not(crossed & (y == 1)))
 
     def second_up_valid(c):
         valid = (y < 3) & (chip >= 1)
@@ -328,7 +339,7 @@
         def _():
             far(c).wait_recv()
             when(up_relay, lambda: up(c).start())
-            when(down_relay, lambda: down(c).start())
+            when(down_valid(c) & (y > 0), lambda: down(c).start())
             when(core == 1, lambda: to_sibling(c, 8).start())
 
     def relay_up(c):
@@ -560,7 +571,7 @@
         if c[1] < PART:
             when(goes_across, lambda: across(c).wait_send())
         when(up_own | up_relay, lambda: up(c).wait_send())
-        when(down_own | down_relay, lambda: down(c).wait_send())
+        when(down_valid(c), lambda: down(c).wait_send())
         when(second_up_valid(c), lambda: second_up(c).wait_send())
         when(second_down_valid(c), lambda: second_down(c).wait_send())
         for slot in (0, 2, 4, 6, 8):

time: 113 us -> 111 us (0.982); the launches traced: 113 us -> 109 us
  Pallas kernels: 110 us -> 106 us
    pallas_call x1, Pallas kernels: 110 us -> 106 us  [local(): pl.pallas_call(layer_kernel, out_shape=jax.ShapeDtypeStruct((ROWS, HALF),...]
where the time goes in v5:
time: 111 us; the launch traced here: 109 us
  Pallas kernels  106 us (95%)
  local copies, waits for them, and re-layouts  2.85 us (3%)
    pallas_call x1, Pallas kernels, local(): pl.pallas_call(layer_kernel, out_shape=jax.ShapeDtypeStruct((ROWS, HALF),...  106 us
    unnamed x1, local copies, waits for them, and re-layouts  2.85 us

profile of v5, /device:TPU:64, one launch (start us, length us, event | category | flops | bytes accessed | tf_op | source)
XLA Modules:
  0.0 109.3 jit_solution(1901900706401303277)
XLA Ops:
  0.0 106.4 %layer.1 = bf16[512,1792]{1,0:T(8,128)(2,1)} custom-call(bf16[512,1792]{1,0:T(8,128)(2,1)} %tok.1, f32[3584]{0:T(1024)} %gain.1, bf16[3584,1024]{1,0:T(8,128)(2,1)} %wq.1, bf16[3584,512]{1,0:T(8,128)(2,1)} %wk.1, bf16[3584,512]{1,0:T(8,128)(2,1)} %wv.1, bf16[1024,3584]{1,0:T(8,128)(2,1)} %wo.1, f32[1792]{0:T(1024)} %post.1, ...), custom_call_target="tpu_custom_call" | custom-call | tf_op jit(solution)/shard_map/layer/pallas_call | solution.py:612
  106.4 2.8 %copy.11 = bf16[512,1792]{1,0:T(8,128)(2,1)} copy(bf16[512,1792]{1,0:T(8,128)(2,1)} %layer.1) | data formatting | bytes 3670016

commit v6 on v5

--- a/solution.py
+++ b/solution.py
@@ -204,7 +204,7 @@
         )
 
     def column_of(c):
-        return jnp.where(c[0] < LONG - 1, lax.rem(c[0], 3), jnp.where(c[0] == LONG - 1, 1, 0))
+        return jnp.where(c[0] < LONG - 1, lax.rem(c[0], 3), jnp.where(c[0] == LONG - 1, 3, 0))
 
     def in_own_column(c):
         return column_of(c) == 0
@@ -435,9 +435,15 @@
                 add([block(1 + j, None)], False)
                 return carry
 
-            lax.fori_loop(0, jnp.minimum(7, s), single, 0)
-
-    late = crossed | crosses
+            def triple(j, carry):
+                add([block(1 + 3 * j + k, None) for k in range(3)], False)
+                return carry
+
+            triples = lax.div(s, 3)
+            lax.fori_loop(0, triples, triple, 0)
+            lax.fori_loop(3 * triples, jnp.minimum(7, s), single, 0)
+
+    late = has_prev
     far_lag = jnp.where(crossed, 2, 1)
     near_lag = jnp.where(far_lag == 1, 2, far_lag + 1)
     up_lag = jnp.where(y == 0, near_lag, 2)
@@ -456,7 +462,7 @@
 
     def step(t, carry):
         each_chunk(t, jnp.minimum(t + 1, CHUNKS), own)
-        each_chunk(jnp.maximum(t - 1, 0), jnp.minimum(t, CHUNKS), relay_onward)
+        each_chunk(jnp.maximum(t - 2, 0), jnp.clip(t - 1, 0, CHUNKS), relay_onward)
         relay(t, far_lag, 0, relay_far)
         relay(t, up_lag, 1, relay_up)
         relay(t, down_lag, 1, relay_down)

time: 111 us -> 111 us (level); the launches traced: 109 us -> 110 us
  Pallas kernels: 106 us -> 108 us
    pallas_call x1, Pallas kernels: 106 us -> 108 us  [local(): pl.pallas_call(layer_kernel, out_shape=jax.ShapeDtypeStruct((ROWS, HALF),...]
where the time goes in v6:
time: 111 us; the launch traced here: 110 us
  Pallas kernels  108 us (97%)
  local copies, waits for them, and re-layouts  2.85 us (3%)
    pallas_call x1, Pallas kernels, local(): pl.pallas_call(layer_kernel, out_shape=jax.ShapeDtypeStruct((ROWS, HALF),...  108 us
    unnamed x1, local copies, waits for them, and re-layouts  2.85 us

profile of v6, /device:TPU:64, one launch (start us, length us, event | category | flops | bytes accessed | tf_op | source)
XLA Modules:
  0.0 110.4 jit_solution(39802618246141083)
XLA Ops:
  0.0 107.5 %layer.1 = bf16[512,1792]{1,0:T(8,128)(2,1)} custom-call(bf16[512,1792]{1,0:T(8,128)(2,1)} %tok.1, f32[3584]{0:T(1024)} %gain.1, bf16[3584,1024]{1,0:T(8,128)(2,1)} %wq.1, bf16[3584,512]{1,0:T(8,128)(2,1)} %wk.1, bf16[3584,512]{1,0:T(8,128)(2,1)} %wv.1, bf16[1024,3584]{1,0:T(8,128)(2,1)} %wo.1, f32[1792]{0:T(1024)} %post.1, ...), custom_call_target="tpu_custom_call" | custom-call | tf_op jit(solution)/shard_map/layer/pallas_call | solution.py:618
  107.6 2.8 %copy.11 = bf16[512,1792]{1,0:T(8,128)(2,1)} copy(bf16[512,1792]{1,0:T(8,128)(2,1)} %layer.1) | data formatting | bytes 3670016
